TPU v7x, 8 devices: a whole 2x2x1 slice. The times are simulated.
8 devices in a mesh: replica: 2 (over z, y), model: 4 (over x, core).
Axes of the slice: x: 2, y: 2, z: 1, core: 2. Of those that a mesh axis runs over, the one named last changes fastest.
Arguments:
- x: bfloat16 [128, 8192], P('replica'), parts along dimension 0
- cache_len: int32 [128], P('replica'), parts along dimension 0
- w_query: bfloat16 [2, 8192, 8192], P(None, None, 'model')
- w_key: bfloat16 [2, 8192, 128], replicated
- w_value: bfloat16 [2, 8192, 128], replicated
- w_out: bfloat16 [2, 8192, 8192], P(None, 'model')
- k_cache: bfloat16 [2, 128, 2048, 128], P(None, ('replica', 'model')), parts along dimension 1
- v_cache: bfloat16 [2, 128, 2048, 128], P(None, ('replica', 'model')), parts along dimension 1
Outputs:
- output 1: bfloat16 [128, 8192], P('replica'), parts along dimension 0
- output 2: bfloat16 [2, 128, 2048, 128], P(None, ('replica', 'model')), parts along dimension 1
- output 3: bfloat16 [2, 128, 2048, 128], P(None, ('replica', 'model')), parts along dimension 1
There are 2 independent parts. A program takes and returns all parts, laid end to end along the dimension named above; an argument that names none is the same for every part.
All inputs are finite; a program needn't handle non-finite values.
Results may differ from a plain program's by a relative error of at most 0.00572.
Values are sent between devices in bfloat16 or wider.
A program may use at most 1 GiB of HBM per device.

v0:
```python
import functools

import jax
import jax.numpy as jnp
from jax import lax
from jax.experimental import pallas as pl
from jax.experimental.pallas import tpu as pltpu
from jax.sharding import PartitionSpec as P

F32 = jnp.float32
BF16 = jnp.bfloat16
MIB = 1 << 20
BIG = 50 * MIB

GROUPS = 4
ROWS = 64
MINE = 16
D = 8192
HD = 128
LH = 16
QW = LH * HD
SEQ = 2048
CH = 512
NJ = QW // CH
QKV = QW + 2 * HD
WO_SLOTS = 6
BLK = 256
VM = pltpu.VMEM
VSPEC = pl.BlockSpec(memory_space=pltpu.VMEM)
ASPEC = pl.BlockSpec(memory_space=pltpu.HBM)
SSPEC = pl.BlockSpec(memory_space=pltpu.SMEM)


def sds(shape, dtype=BF16):
    return jax.ShapeDtypeStruct(shape, dtype)


def qkv_copies(layer, chunk, slot, wq, wk, wv, buf, sems):
    rows = pl.ds(pl.multiple_of(chunk * CH, CH), CH)
    return (
        pltpu.make_async_copy(wq.at[layer, rows, :], buf.at[slot, :, pl.ds(0, QW)], sems.at[0, slot]),
        pltpu.make_async_copy(wk.at[layer, rows, :], buf.at[slot, :, pl.ds(QW, HD)], sems.at[1, slot]),
        pltpu.make_async_copy(wv.at[layer, rows, :], buf.at[slot, :, pl.ds(QW + HD, HD)], sems.at[2, slot]),
    )


def write_qkv(me, acc, q_outs, k_new, v_new):
    for i, q_out in enumerate(q_outs):
        other = xor_id(me, i)
        q_out[...] = acc[pl.ds(pl.multiple_of(other * MINE, MINE), MINE), 0:QW].astype(BF16)
    mine = pl.ds(pl.multiple_of(me * MINE, MINE), MINE)
    k_new[...] = acc[mine, QW:QW + HD].astype(BF16)
    v_new[...] = acc[mine, QW + HD:QKV].astype(BF16)


def xor_id(me, i):
    core = lax.rem(me, 2)
    other = me
    if i & 1:
        other = other + 1 - 2 * core
    if i & 2:
        other = lax.rem(other + 2, GROUPS)
    return other


def first_qkv_kernel(x, wq, wk, wv, q0, q1, q2, q3, k_new, v_new, buf, acc, xbuf, sems, x_sem):
    me = lax.axis_index("model")
    chunks = D // CH
    x_copy = pltpu.make_async_copy(x, xbuf, x_sem)
    x_copy.start()

    def start(c, _):
        for cp in qkv_copies(0, c, c, wq, wk, wv, buf, sems):
            cp.start()
        return 0

    lax.fori_loop(0, chunks, start, 0)
    acc[...] = jnp.zeros_like(acc)
    x_copy.wait()

    def step(c, _):
        for cp in qkv_copies(0, c, c, wq, wk, wv, buf, sems):
            cp.wait()
        cols = pl.ds(pl.multiple_of(c * CH, CH), CH)
        acc[...] += jnp.dot(xbuf[:, cols], buf[c], preferred_element_type=F32)
        return 0

    lax.fori_loop(0, chunks, step, 0)
    write_qkv(me, acc, (q0, q1, q2, q3), k_new, v_new)


def first_qkv(x, wq, wk, wv):
    n = D // CH
    return pl.pallas_call(
        first_qkv_kernel,
        out_shape=[sds((MINE, QW))] * 4 + [sds((MINE, HD))] * 2,
        in_specs=[ASPEC] * 4,
        out_specs=[VSPEC] * 6,
        scratch_shapes=[
            VM((n, CH, QKV), BF16),
            VM((ROWS, QKV), F32),
            VM((ROWS, D), BF16),
            pltpu.SemaphoreType.DMA((3, n)),
            pltpu.SemaphoreType.DMA,
        ],
        compiler_params=pltpu.CompilerParams(vmem_limit_bytes=BIG),
        cost_estimate=pl.CostEstimate(flops=2 * ROWS * D * QKV, bytes_accessed=2 * D * QKV, transcendentals=0),
        name="first_qkv",
    )(x, wq, wk, wv)


K_CUT = 6
V_CUT = 10


def put_row(buf, b, length, row):
    base = pl.multiple_of((length // 16) * 16, 16)
    here = lax.broadcasted_iota(jnp.int32, (16, HD), 0) == length - base
    buf[b, pl.ds(base, 16), :] = jnp.where(here, row, buf[b, pl.ds(base, 16), :])


class Share:
    def __init__(self, layer, first, last, lens, new, src, dst, buf, in_sems, out_sems):
        self.layer, self.first, self.count = layer, first, last - first
        self.lens, self.new, self.src, self.dst, self.buf = lens, new, src, dst, buf
        self.in_sems, self.out_sems = in_sems, out_sems

    def take(self, n):
        return pltpu.make_async_copy(self.src.at[self.layer, self.first + n], self.buf.at[n], self.in_sems.at[n])

    def give(self, n):
        return pltpu.make_async_copy(self.buf.at[n], self.dst.at[self.layer, self.first + n], self.out_sems.at[n])

    def start(self):
        for n in range(self.count):
            self.take(n).start()

    def forward(self):
        me = lax.axis_index("model")
        for n in range(self.count):
            self.take(n).wait()
            b = self.first + n
            put_row(self.buf, n, self.lens[me * MINE + b], self.new[pl.ds(b, 1), :])
            if n:
                self.give(n - 1).start()
        self.give(self.count - 1).start()

    def finish(self):
        for n in range(self.count):
            self.give(n).wait()

    @staticmethod
    def scratch(first, last):
        return [VM((last - first, SEQ, HD), BF16), pltpu.SemaphoreType.DMA((last - first,)),
                pltpu.SemaphoreType.DMA((last - first,))]


def copy_kernel(layer, first, last, n_in, *refs):
    lens, new, src = refs[:3]
    share = Share(layer, first, last, lens, new, src, *refs[n_in:])
    share.start()
    share.forward()
    share.finish()


def copy_cache(layer, first, last, lens, new, src, prior):
    args = [lens, new, src] + ([prior] if prior is not None else [])
    return pl.pallas_call(
        functools.partial(copy_kernel, layer, first, last, len(args)),
        out_shape=sds(src.shape),
        in_specs=[SSPEC, VSPEC, ASPEC] + ([ASPEC] if prior is not None else []),
        out_specs=ASPEC,
        input_output_aliases={3: 0} if prior is not None else {},
        scratch_shapes=Share.scratch(first, last),
        compiler_params=pltpu.CompilerParams(vmem_limit_bytes=BIG),
        cost_estimate=pl.CostEstimate(flops=5_000_000_000, bytes_accessed=4 * MINE * SEQ * HD, transcendentals=0),
        name=f"copy_cache_{layer}",
    )(*args)


GRP = 4
TIERS = (512, 1024, 2048)


def attend_kernel(layer, n_in, *refs):
    lens, r0, r1, r2, r3, k_new, v_new, k_cache, v_cache = refs[:9]
    c0, c1, c2, c3, k_out, v_out, kbuf, vbuf, qbuf, cbuf, new_kv, ksems, vsems = refs[n_in:n_in + 13]
    shares = refs[n_in + 13:]
    k_share = Share(layer, K_CUT, MINE, lens, k_new, k_cache, k_out, *shares[:3])
    v_share = Share(layer, 0, V_CUT, lens, v_new, v_cache, v_out, *shares[3:])
    me = lax.axis_index("model")
    n_heads = GROUPS * LH
    scale = HD ** -0.5

    def length(b):
        return lens[me * MINE + b]

    def tier_of(b, n):
        return jnp.logical_and(length(b) < TIERS[n], length(b) >= (TIERS[n - 1] if n else BLK))

    def copies(b, part):
        cut = pl.ds(*part)
        return (pltpu.make_async_copy(k_cache.at[layer, b, cut, :], kbuf.at[b, cut, :], ksems.at[b, part[0] // BLK]),
                pltpu.make_async_copy(v_cache.at[layer, b, cut, :], vbuf.at[b, cut, :], vsems.at[b, part[0] // BLK]))

    def start_first(b, _):
        for cp in copies(b, (0, BLK)):
            cp.start()
        return 0

    def start_rest(b, _):
        for n, size in enumerate(TIERS):
            @pl.when(tier_of(b, n))
            def _(size=size):
                for cp in copies(b, (BLK, size - BLK)):
                    cp.start()
        return 0

    lax.fori_loop(0, MINE, start_first, 0)
    lax.fori_loop(0, MINE, start_rest, 0)
    k_share.start()
    v_share.start()

    for i, r in enumerate((r0, r1, r2, r3)):
        qbuf[:, i * LH:(i + 1) * LH, :] = r[...].reshape(MINE, LH, HD)

    for b in range(MINE):
        new_kv[0, b] = k_new[b:b + 1, :].astype(F32)
        new_kv[1, b] = v_new[b:b + 1, :].astype(F32)

    def new_rows(b):
        put_row(kbuf, b, length(b), new_kv[0, b].astype(BF16))
        put_row(vbuf, b, length(b), new_kv[1, b].astype(BF16))

    def context(seqs, size):
        scores = []
        for b in seqs:
            s = lax.dot_general(qbuf[b], kbuf[b, 0:size, :], (((1,), (1,)), ((), ())),
                                preferred_element_type=F32)
            pos = lax.broadcasted_iota(jnp.int32, (n_heads, size), 1)
            scores.append(jnp.where(pos <= length(b), s * scale, -jnp.inf))
        expos = [jnp.exp(s - jnp.max(s, axis=1, keepdims=True)) for s in scores]
        probs = [(e * (1.0 / jnp.sum(e, axis=1, keepdims=True))).astype(BF16) for e in expos]
        for b, p in zip(seqs, probs):
            cbuf[b] = jnp.dot(p, vbuf[b, 0:size, :], preferred_element_type=F32).astype(BF16)

    def first_blocks(g, _):
        seqs = [g * GRP + i for i in range(GRP)]
        for b in seqs:
            for cp in copies(b, (0, BLK)):
                cp.wait()

            @pl.when(length(b) < BLK)
            def _(b=b):
                new_rows(b)
        context(seqs, BLK)
        return 0

    lax.fori_loop(0, MINE // GRP, first_blocks, 0)
    k_share.forward()
    v_share.forward()

    def rest(b, _):
        for n, size in enumerate(TIERS):
            @pl.when(tier_of(b, n))
            def _(size=size):
                for cp in copies(b, (BLK, size - BLK)):
                    cp.wait()
                new_rows(b)
                context((b,), size)
        return 0

    lax.fori_loop(0, MINE, rest, 0)

    for i, c in enumerate((c0, c1, c2, c3)):
        c[...] = cbuf[:, i * LH:(i + 1) * LH, :].reshape(MINE, QW)
    k_share.finish()
    v_share.finish()


def attend(layer, lens, rs, k_new, v_new, k_cache, v_cache, k_out, v_out):
    args = [lens, *rs, k_new, v_new, k_cache, v_cache, k_out] + ([v_out] if v_out is not None else [])
    return pl.pallas_call(
        functools.partial(attend_kernel, layer, len(args)),
        out_shape=[sds((MINE, QW))] * 4 + [sds(k_cache.shape)] * 2,
        in_specs=[SSPEC] + [VSPEC] * 6 + [ASPEC] * (len(args) - 7),
        out_specs=[VSPEC] * 4 + [ASPEC] * 2,
        input_output_aliases={9: 4} if v_out is None else {9: 4, 10: 5},
        scratch_shapes=[
            VM((MINE, SEQ, HD), BF16),
            VM((MINE, SEQ, HD), BF16),
            VM((MINE, GROUPS * LH, HD), BF16),
            VM((MINE, GROUPS * LH, HD), BF16),
            VM((2, MINE, 1, HD), F32),
            pltpu.SemaphoreType.DMA((MINE, 2)),
            pltpu.SemaphoreType.DMA((MINE, 2)),
            *Share.scratch(K_CUT, MINE),
            *Share.scratch(0, V_CUT),
        ],
        compiler_params=pltpu.CompilerParams(vmem_limit_bytes=BIG),
        cost_estimate=pl.CostEstimate(flops=5_000_000_000, bytes_accessed=8 * MIB, transcendentals=0),
        name=f"attend_{layer}",
    )(*args)


def out_kernel(layer, fuse, *refs):
    d_refs, (res, wo), refs = refs[:4], refs[4:6], refs[6:]
    if fuse:
        (wq, wk, wv), outs, refs = refs[:3], refs[3:10], refs[10:]
        q_outs, (k_new, v_new, res_out) = outs[:4], outs[4:]
        hid, qbuf, acc, q_sems = refs[:4]
        refs = refs[4:]
    else:
        hid, refs = refs[0], refs[1:]
    ctx, resv, wbuf, send_a, recv_a, send_c, recv_c, send_b, recv_b, own, w_sems, res_sem, ssems, rsems = refs

    me = lax.axis_index("model")
    partner, cross, diag = xor_id(me, 1), xor_id(me, 2), xor_id(me, 3)

    def cols(chunk):
        return pl.ds(pl.multiple_of(chunk * CH, CH), CH)

    def wo_copy(step):
        chip_of = lax.rem(lax.div(me, 2) + 1 - step // (2 * NJ), 2)
        core_of = lax.rem(lax.rem(me, 2) + 1 - step % 2, 2)
        chunk = (chip_of * 2 + core_of) * NJ + step % (2 * NJ) // 2
        slot = step % WO_SLOTS
        return pltpu.make_async_copy(wo.at[layer, :, cols(chunk)], wbuf.at[slot], w_sems.at[slot])

    def q_copies(chunk, slot):
        return qkv_copies(layer + 1, chunk, slot, wq, wk, wv, qbuf, q_sems)

    def send(kind, j, src, dst, dev):
        return pltpu.make_async_remote_copy(
            src_ref=src, dst_ref=dst, send_sem=ssems.at[kind, j], recv_sem=rsems.at[kind, j],
            device_id={"model": dev}, device_id_type=pl.DeviceIdType.MESH)

    def pair_a(j):
        return send(0, j, send_a.at[j], recv_a.at[j], partner)

    def pair_b(j):
        return send(1, j, send_b.at[j], recv_b.at[j], partner)

    def across(j):
        return send(2, j, send_c.at[j], recv_c.at[j], cross)

    def hidden(kind, j, owner, dev):
        part = hid.at[:, cols(owner * NJ + j)]
        return send(kind, j, part, part, dev)

    def start_wo(step, _):
        wo_copy(step).start()
        return 0

    lax.fori_loop(0, WO_SLOTS, start_wo, 0)
    if fuse:
        res_copy = pltpu.make_async_copy(
            res.at[:, pl.ds(pl.multiple_of(me * QW, QW), QW)], resv, res_sem)
    else:
        res_copy = pltpu.make_async_copy(res, resv, res_sem)
    res_copy.start()

    for i, d in enumerate(d_refs):
        ctx[pl.ds(pl.multiple_of(xor_id(me, i) * MINE, MINE), MINE), :] = d[...]
    if fuse:
        acc[...] = jnp.zeros_like(acc)

    barrier = pltpu.get_barrier_semaphore()
    for dev in (partner, cross):
        pl.semaphore_signal(barrier, inc=1, device_id={"model": dev}, device_id_type=pl.DeviceIdType.MESH)
    pl.semaphore_wait(barrier, 2)

    def part_sum(step):
        wo_copy(step).wait()
        return jnp.dot(ctx[...], wbuf[step % WO_SLOTS], preferred_element_type=F32)

    def refill(step):
        @pl.when(step + WO_SLOTS < 4 * NJ)
        def _():
            wo_copy(step + WO_SLOTS).start()

    def send_across(j):
        pair_a(j).wait_recv()
        send_c[j] += recv_a[j]
        across(j).start()

    def phase_a(j, _):
        send_a[j] = part_sum(2 * j)
        pair_a(j).start()
        refill(2 * j)

        @pl.when(j > 0)
        def _():
            send_across(j - 1)
        send_c[j] = part_sum(2 * j + 1)
        refill(2 * j + 1)
        return 0

    lax.fori_loop(0, NJ, phase_a, 0)
    send_across(NJ - 1)

    def phase_b(j, _):
        step = 2 * NJ + 2 * j
        send_b[j] = part_sum(step)
        pair_b(j).start()
        refill(step)
        own[j] = part_sum(step + 1)
        refill(step + 1)
        if fuse:
            for i, owner in enumerate((me, partner)):
                for cp in q_copies(owner * NJ + j, 2 * j + i):
                    cp.start()
        return 0

    lax.fori_loop(0, NJ, phase_b, 0)
    if fuse:
        def start_far(j, _):
            for i, owner in enumerate((cross, diag)):
                for cp in q_copies(owner * NJ + j, 2 * NJ + 2 * j + i):
                    cp.start()
            return 0

        lax.fori_loop(0, NJ, start_far, 0)
    res_copy.wait()

    def next_q(owner, j, slot):
        if fuse:
            chunk = owner * NJ + j
            for cp in q_copies(chunk, slot):
                cp.wait()
            acc[...] += jnp.dot(hid[:, cols(chunk)], qbuf[slot], preferred_element_type=F32)

    def from_partner(j):
        hidden(3, j, partner, partner).wait_recv()
        next_q(partner, j, 2 * j + 1)

    def phase_c(j, _):
        pair_b(j).wait_recv()
        across(j).wait_recv()
        total = own[j] + recv_b[j] + recv_c[j]
        part = (resv[:, cols(j)].astype(F32) + total).astype(BF16)
        hid[:, cols(me * NJ + j)] = part
        if fuse:
            res_out[:, cols(j)] = part
        hidden(4, j, me, cross).start()
        hidden(3, j, me, partner).start()
        next_q(me, j, 2 * j)

        @pl.when(j > 0)
        def _():
            from_partner(j - 1)
        return 0

    lax.fori_loop(0, NJ, phase_c, 0)
    from_partner(NJ - 1)

    def forwarded(j):
        hidden(5, j, diag, partner).wait_recv()
        next_q(diag, j, 2 * NJ + 2 * j + 1)

    def phase_d(j, _):
        hidden(4, j, cross, cross).wait_recv()
        hidden(5, j, cross, partner).start()
        next_q(cross, j, 2 * NJ + 2 * j)

        @pl.when(j > 0)
        def _():
            forwarded(j - 1)
        return 0

    lax.fori_loop(0, NJ, phase_d, 0)
    forwarded(NJ - 1)

    if fuse:
        write_qkv(me, acc, q_outs, k_new, v_new)

    def drain(j, _):
        pair_a(j).wait_send()
        pair_b(j).wait_send()
        across(j).wait_send()
        hidden(3, j, me, partner).wait_send()
        hidden(4, j, me, cross).wait_send()
        hidden(5, j, cross, partner).wait_send()
        return 0

    lax.fori_loop(0, NJ, drain, 0)


def out_product(layer, fuse, ds, res, w_out, qkv_weights):
    part = (NJ, ROWS, CH)
    shared = [
        VM((ROWS, QW), BF16),
        VM((ROWS, QW), BF16),
        VM((WO_SLOTS, QW, CH), BF16),
        VM(part, F32), VM(part, F32), VM(part, F32), VM(part, F32), VM(part, F32), VM(part, F32), VM(part, F32),
        pltpu.SemaphoreType.DMA((WO_SLOTS,)),
        pltpu.SemaphoreType.DMA,
        pltpu.SemaphoreType.DMA((6, NJ)),
        pltpu.SemaphoreType.DMA((6, NJ)),
    ]
    n = D // CH
    flops = 2 * ROWS * QW * D
    if fuse:
        out_shape = [sds((MINE, QW))] * 4 + [sds((MINE, HD))] * 2 + [sds((ROWS, QW))]
        out_specs = [VSPEC] * 7
        extra = [
            VM((ROWS, D), BF16),
            VM((n, CH, QKV), BF16),
            VM((ROWS, QKV), F32),
            pltpu.SemaphoreType.DMA((3, n)),
        ]
        args = (*ds, res, w_out, *qkv_weights)
        flops += 2 * ROWS * D * QKV
    else:
        out_shape = sds((ROWS, D))
        out_specs = VSPEC
        extra = []
        args = (*ds, res, w_out)
    return pl.pallas_call(
        functools.partial(out_kernel, layer, fuse),
        out_shape=out_shape,
        in_specs=[VSPEC] * 4 + [ASPEC] * (len(args) - 4),
        out_specs=out_specs,
        scratch_shapes=extra + shared,
        compiler_params=pltpu.CompilerParams(
            vmem_limit_bytes=58 * MIB if fuse else 32 * MIB, collective_id=layer, has_side_effects=True),
        cost_estimate=pl.CostEstimate(flops=flops, bytes_accessed=flops // ROWS, transcendentals=0),
        name=f"out_product_{layer}",
    )(*args)


def swap(parts):
    out = [parts[0]]
    for i in range(1, GROUPS):
        out.append(lax.ppermute(parts[i], "model", [(m, m ^ i) for m in range(GROUPS)]))
    return out


def solution(mesh):
    cache_spec = P(None, ("replica", "model"), None, None)

    def device_step(x, cache_len, w_query, w_key, w_value, w_out, k_cache, v_cache):
        *qs, k_new, v_new = first_qkv(x, w_query, w_key, w_value)
        k_out = v_out = None
        res = x
        for layer in range(2):
            rs = swap(qs)
            k_out = copy_cache(layer, 0, K_CUT, cache_len, k_new, k_cache, k_out)
            *cs, k_out, v_out = attend(layer, cache_len, rs, k_new, v_new, k_cache, v_cache, k_out, v_out)
            ds = swap(cs)
            v_out = copy_cache(layer, V_CUT, MINE, cache_len, v_new, v_cache, v_out)
            if layer == 0:
                *qs, k_new, v_new, res = out_product(0, True, ds, x, w_out, (w_query, w_key, w_value))
            else:
                out = out_product(1, False, ds, res, w_out, ())
        return out, k_out, v_out

    return jax.shard_map(
        device_step,
        mesh=mesh,
        in_specs=(P("replica", None), P("replica"), P(None, None, "model"), P(), P(), P(None, "model", None), cache_spec, cache_spec),
        out_specs=(P("replica", None), cache_spec, cache_spec),
        check_vma=False,
    )
```

profile of v0, /device:TPU:0, one launch (start us, length us, event | category | flops | bytes accessed | tf_op | source)
XLA Modules:
  0.0 113.4 jit_solution(8744716395121894982)
XLA Ops:
  0.6 1.2 %copy-done = bf16[64,8192]{1,0:T(8,128)(2,1)S(1)} copy-done((bf16[64,8192]{1,0:T(8,128)(2,1)S(1)}, bf16[64,8192]{1,0:T(8,128)(2,1)}, u32[]{:S(2)}) %copy-start) | copy-done | bytes 1048600
  1.9 12.9 %first_qkv.1 = (bf16[16,2048]{1,0:T(8,128)(2,1)S(1)}, bf16[16,2048]{1,0:T(8,128)(2,1)S(1)}, bf16[16,2048]{1,0:T(8,128)(2,1)S(1)}, bf16[16,2048]{1,0:T(8,128)(2,1...) custom-call(bf16[64,8192]{1,0:T(8,128)(2,1)S(1)} %copy-done, bf16[2,8192,2048]{2,1,0:T(8,128)(2,1)} %refs_6_.1, ...), custom_call_target="tpu_custom_call" | custom-call | flops 2415919104 | bytes 37748736 | tf_op jit(solution)/shard_map/first_qkv/pallas_call | solution.py:94
  14.7 0.9 collective-permute-start
  15.6 2.5 %collective-permute-start.1 = (bf16[16,2048]{1,0:T(8,128)(2,1)S(1)}, bf16[16,2048]{1,0:T(8,128)(2,1)S(1)}, u32[]{:S(2)}, u32[]{:S(2)}) collective-permute-start(bf16[16,2048]{1,0:T(8,128)(2,1)S(1)} %get-tuple-element.30), channel_id=1, source_target_pairs={{0,2},{1,3},{2,0},{3,1},{4,6},{5,7},{6,4},{7,5}} | collective-permute-start | bytes 196616 | tf_op jit(solution)/shard_map/ppermute | solution.py:535
  18.2 3.5 %copy_cache_0.2.refs_9_ = bf16[2,16,2048,128]{3,2,1,0:T(8,128)(2,1)} custom-call(s32[64]{0:T(128)S(1)} %copy-done.4, bf16[16,128]{1,0:T(8,128)(2,1)S(1)} %get-tuple-element.32.refs_1_.refs_5_, bf16[2,16,2048,128]{3,2,1,0:T(8,128)(2,1)} %refs_7_.5), custom_call_target="tpu_custom_call" | custom-call | flops 5000000000 | bytes 16777216 | tf_op jit(solution)/shard_map/copy_cache_0/pallas_call | solution.py:168
  21.7 0.4 collective-permute-done.2.refs_4_
  22.1 10.3 %attend_0.1 = (bf16[16,2048]{1,0:T(8,128)(2,1)S(1)}, bf16[16,2048]{1,0:T(8,128)(2,1)S(1)}, bf16[16,2048]{1,0:T(8,128)(2,1)S(1)}, bf16[16,2048]{1,0:T(8,128)(2,1)...) custom-call(s32[64]{0:T(128)S(1)} %copy-done.4, ...), custom_call_target="tpu_custom_call", output_to_operand_aliasing={{4}: (9, {})} | custom-call | flops 5000000000 | bytes 8388608 | tf_op jit(solution)/shard_map/attend_0/pallas_call | solution.py:283
  32.4 0.7 collective-permute-start.3
  33.2 0.9 collective-permute-start.4
  34.1 0.4 collective-permute-start.5
  34.6 3.5 %copy_cache_0.3.refs_10_ = bf16[2,16,2048,128]{3,2,1,0:T(8,128)(2,1)} custom-call(s32[64]{0:T(128)S(1)} %copy-done.4, bf16[16,128]{1,0:T(8,128)(2,1)S(1)} %get-tuple-element.33.refs_6_.refs_1_, bf16[2,16,2048,128]{3,2,1,0:T(8,128)(2,1)} %refs_2_.7, bf16[2,16,2048,128]{3,2,1,0:T(8,128)(2,1)} %get-tuple-element.45.refs_3_), custom_call_target="tpu_custom_call", output_to_operand_aliasing={{}: (3, {})} | custom-call | flops 5000000000 | bytes 16777216 | tf_op jit(solution)/shard_map/copy_cache_0/pallas_call | solution.py:168
  38.7 0.4 copy-done.9
  39.1 26.9 %out_product_0.1 = (bf16[16,2048]{1,0:T(8,128)(2,1)}, bf16[16,2048]{1,0:T(8,128)(2,1)}, bf16[16,2048]{1,0:T(8,128)(2,1)}, bf16[16,2048]{1,0:T(8,128)(2,1)}, bf16...) custom-call(bf16[16,2048]{1,0:T(8,128)(2,1)} %copy-done.2, bf16[16,2048]{1,0:T(8,128)(2,1)} %copy-done.7, ...), custom_call_target="tpu_custom_call" | custom-call | flops 4563402752 | bytes 71303168 | tf_op jit(solution)/shard_map/out_product_0/pallas_call | solution.py:519
  66.2 1.0 collective-permute-start.7
  67.2 0.7 collective-permute-start.8
  67.9 0.7 copy-done.6
  68.6 3.5 %copy_cache_1.2.refs_9_ = bf16[2,16,2048,128]{3,2,1,0:T(8,128)(2,1)} custom-call(s32[64]{0:T(128)S(1)} %copy-done.4, bf16[16,128]{1,0:T(8,128)(2,1)S(1)} %copy-done.6, bf16[2,16,2048,128]{3,2,1,0:T(8,128)(2,1)} %refs_7_.5, bf16[2,16,2048,128]{3,2,1,0:T(8,128)(2,1)} %get-tuple-element.44.refs_3_), custom_call_target="tpu_custom_call", output_to_operand_aliasing={{}: (3, {})} | custom-call | flops 5000000000 | bytes 16777216 | tf_op jit(solution)/shard_map/copy_cache_1/pallas_call | solution.py:168
  72.2 10.3 %attend_1.1 = (bf16[16,2048]{1,0:T(8,128)(2,1)S(1)}, bf16[16,2048]{1,0:T(8,128)(2,1)S(1)}, bf16[16,2048]{1,0:T(8,128)(2,1)S(1)}, bf16[16,2048]{1,0:T(8,128)(2,1)...) custom-call(s32[64]{0:T(128)S(1)} %copy-done.4, ...), custom_call_target="tpu_custom_call", output_to_operand_aliasing={{4}: (9, {}), {5}: (10, {})} | custom-call | flops 5000000000 | bytes 8388608 | tf_op jit(solution)/shard_map/attend_1/pallas_call | solution.py:283
  82.5 0.8 collective-permute-start.9
  83.3 0.9 collective-permute-start.10
  84.2 0.5 collective-permute-start.11
  84.7 3.5 %copy_cache_1.3 = bf16[2,16,2048,128]{3,2,1,0:T(8,128)(2,1)} custom-call(s32[64]{0:T(128)S(1)} %copy-done.4, bf16[16,128]{1,0:T(8,128)(2,1)S(1)} %copy-done.5, bf16[2,16,2048,128]{3,2,1,0:T(8,128)(2,1)} %refs_2_.7, bf16[2,16,2048,128]{3,2,1,0:T(8,128)(2,1)} %get-tuple-element.52.refs_3_), custom_call_target="tpu_custom_call", output_to_operand_aliasing={{}: (3, {})} | custom-call | flops 5000000000 | bytes 16777216 | tf_op jit(solution)/shard_map/copy_cache_1/pallas_call | solution.py:168
  88.6 23.8 %out_product_1.1 = bf16[64,8192]{1,0:T(8,128)(2,1)S(1)} custom-call(bf16[16,2048]{1,0:T(8,128)(2,1)S(1)} %get-tuple-element.46.refs_0_, bf16[16,2048]{1,0:T(8,128)(2,1)S(1)} %collective-permute-done.9.refs_1_, bf16[16,2048]{1,0:T(8,128)(2,1)S(1)} %collective-permute-done.10.refs_2_, bf16[16,2048]{1,0:T(8,128)(2,1)S(1)} %collective-permute-done.11.refs_3_, ...), custom_call_target="tpu_custom_call" | custom-call | flops 2147483648 | bytes 33554432 | tf_op jit(solution)/shard_map/out_product_1/pallas_call | solution.py:519
  112.4 1.0 copy.24
  (30 shorter events, 1.3 us)
Async XLA Ops:
  0.6 1.2 %copy-start = (bf16[64,8192]{1,0:T(8,128)(2,1)S(1)}, bf16[64,8192]{1,0:T(8,128)(2,1)}, u32[]{:S(2)}) copy-start(bf16[64,8192]{1,0:T(8,128)(2,1)} %refs_4_.1) | copy-start | bytes 3145732
  1.9 16.3 %copy-start.4 = (s32[64]{0:T(128)S(1)}, s32[64]{0:T(128)}, u32[]{:S(2)}) copy-start(s32[64]{0:T(128)} %refs_0_.11) | copy-start | bytes 772
  14.7 7.0 %collective-permute-start = (bf16[16,2048]{1,0:T(8,128)(2,1)S(1)}, bf16[16,2048]{1,0:T(8,128)(2,1)S(1)}, u32[]{:S(2)}, u32[]{:S(2)}) collective-permute-start(bf16[16,2048]{1,0:T(8,128)(2,1)S(1)} %get-tuple-element.29), channel_id=1, source_target_pairs={{0,1},{1,0},{2,3},{3,2},{4,5},{5,4},{6,7},{7,6}} | collective-permute-start | bytes 196616 | tf_op jit(solution)/shard_map/ppermute | solution.py:535
  15.6 6.1 %collective-permute-start.1 = (bf16[16,2048]{1,0:T(8,128)(2,1)S(1)}, bf16[16,2048]{1,0:T(8,128)(2,1)S(1)}, u32[]{:S(2)}, u32[]{:S(2)}) collective-permute-start(bf16[16,2048]{1,0:T(8,128)(2,1)S(1)} %get-tuple-element.30), channel_id=1, source_target_pairs={{0,2},{1,3},{2,0},{3,1},{4,6},{5,7},{6,4},{7,5}} | collective-permute-start | bytes 196616 | tf_op jit(solution)/shard_map/ppermute | solution.py:535
  18.1 4.0 %collective-permute-start.2 = (bf16[16,2048]{1,0:T(8,128)(2,1)S(1)}, bf16[16,2048]{1,0:T(8,128)(2,1)S(1)}, u32[]{:S(2)}, u32[]{:S(2)}) collective-permute-start(bf16[16,2048]{1,0:T(8,128)(2,1)S(1)} %get-tuple-element.31), channel_id=1, source_target_pairs={{0,3},{1,2},{2,1},{3,0},{4,7},{5,6},{6,5},{7,4}} | collective-permute-start | bytes 196616 | tf_op jit(solution)/shard_map/ppermute | solution.py:535
  32.4 5.6 %copy-start.2 = (bf16[16,2048]{1,0:T(8,128)(2,1)}, bf16[16,2048]{1,0:T(8,128)(2,1)S(1)}, u32[]{:S(2)}) copy-start(bf16[16,2048]{1,0:T(8,128)(2,1)S(1)} %get-tuple-element.34.refs_0_) | copy-start | bytes 196612
  32.4 5.6 %collective-permute-start.3 = (bf16[16,2048]{1,0:T(8,128)(2,1)S(1)}, bf16[16,2048]{1,0:T(8,128)(2,1)S(1)}, u32[]{:S(2)}, u32[]{:S(2)}) collective-permute-start(bf16[16,2048]{1,0:T(8,128)(2,1)S(1)} %get-tuple-element.35), channel_id=1, source_target_pairs={{0,1},{1,0},{2,3},{3,2},{4,5},{5,4},{6,7},{7,6}} | collective-permute-start | bytes 196616 | tf_op jit(solution)/shard_map/ppermute | solution.py:535
  33.2 4.9 %collective-permute-start.4 = (bf16[16,2048]{1,0:T(8,128)(2,1)S(1)}, bf16[16,2048]{1,0:T(8,128)(2,1)S(1)}, u32[]{:S(2)}, u32[]{:S(2)}) collective-permute-start(bf16[16,2048]{1,0:T(8,128)(2,1)S(1)} %get-tuple-element.36), channel_id=1, source_target_pairs={{0,2},{1,3},{2,0},{3,1},{4,6},{5,7},{6,4},{7,5}} | collective-permute-start | bytes 196616 | tf_op jit(solution)/shard_map/ppermute | solution.py:535
  34.1 4.4 %collective-permute-start.5 = (bf16[16,2048]{1,0:T(8,128)(2,1)S(1)}, bf16[16,2048]{1,0:T(8,128)(2,1)S(1)}, u32[]{:S(2)}, u32[]{:S(2)}) collective-permute-start(bf16[16,2048]{1,0:T(8,128)(2,1)S(1)} %get-tuple-element.37), channel_id=1, source_target_pairs={{0,3},{1,2},{2,1},{3,0},{4,7},{5,6},{6,5},{7,4}} | collective-permute-start | bytes 196616 | tf_op jit(solution)/shard_map/ppermute | solution.py:535
  38.1 0.6 copy-start.7
  38.1 0.6 copy-start.8
  38.5 0.6 copy-start.9
  66.0 6.1 %collective-permute-start.6 = (bf16[16,2048]{1,0:T(8,128)(2,1)}, bf16[16,2048]{1,0:T(8,128)(2,1)S(1)}, u32[]{:S(2)}, u32[]{:S(2)}) collective-permute-start(bf16[16,2048]{1,0:T(8,128)(2,1)} %get-tuple-element.39), channel_id=1, source_target_pairs={{0,1},{1,0},{2,3},{3,2},{4,5},{5,4},{6,7},{7,6}} | collective-permute-start | bytes 196616 | tf_op jit(solution)/shard_map/ppermute | solution.py:535
  66.2 5.9 %collective-permute-start.7 = (bf16[16,2048]{1,0:T(8,128)(2,1)}, bf16[16,2048]{1,0:T(8,128)(2,1)S(1)}, u32[]{:S(2)}, u32[]{:S(2)}) collective-permute-start(bf16[16,2048]{1,0:T(8,128)(2,1)} %get-tuple-element.40), channel_id=1, source_target_pairs={{0,2},{1,3},{2,0},{3,1},{4,6},{5,7},{6,4},{7,5}} | collective-permute-start | bytes 196616 | tf_op jit(solution)/shard_map/ppermute | solution.py:535
  67.2 5.0 %collective-permute-start.8 = (bf16[16,2048]{1,0:T(8,128)(2,1)}, bf16[16,2048]{1,0:T(8,128)(2,1)S(1)}, u32[]{:S(2)}, u32[]{:S(2)}) collective-permute-start(bf16[16,2048]{1,0:T(8,128)(2,1)} %get-tuple-element.41), channel_id=1, source_target_pairs={{0,3},{1,2},{2,1},{3,0},{4,7},{5,6},{6,5},{7,4}} | collective-permute-start | bytes 196616 | tf_op jit(solution)/shard_map/ppermute | solution.py:535
  67.9 0.7 copy-start.6
  68.6 3.6 %copy-start.3 = (bf16[16,2048]{1,0:T(8,128)(2,1)S(1)}, bf16[16,2048]{1,0:T(8,128)(2,1)}, u32[]{:S(2)}) copy-start(bf16[16,2048]{1,0:T(8,128)(2,1)} %get-tuple-element.38.refs_1_) | copy-start | bytes 196612
  68.6 3.6 %copy-start.5 = (bf16[16,128]{1,0:T(8,128)(2,1)S(1)}, bf16[16,128]{1,0:T(8,128)(2,1)}, u32[]{:S(2)}) copy-start(bf16[16,128]{1,0:T(8,128)(2,1)} %get-tuple-element.43.refs_6_.refs_1_) | copy-start | bytes 12292
  82.5 5.7 %collective-permute-start.9 = (bf16[16,2048]{1,0:T(8,128)(2,1)S(1)}, bf16[16,2048]{1,0:T(8,128)(2,1)S(1)}, u32[]{:S(2)}, u32[]{:S(2)}) collective-permute-start(bf16[16,2048]{1,0:T(8,128)(2,1)S(1)} %get-tuple-element.47), channel_id=1, source_target_pairs={{0,1},{1,0},{2,3},{3,2},{4,5},{5,4},{6,7},{7,6}} | collective-permute-start | bytes 196616 | tf_op jit(solution)/shard_map/ppermute | solution.py:535
  83.3 4.9 %collective-permute-start.10 = (bf16[16,2048]{1,0:T(8,128)(2,1)S(1)}, bf16[16,2048]{1,0:T(8,128)(2,1)S(1)}, u32[]{:S(2)}, u32[]{:S(2)}) collective-permute-start(bf16[16,2048]{1,0:T(8,128)(2,1)S(1)} %get-tuple-element.48), channel_id=1, source_target_pairs={{0,2},{1,3},{2,0},{3,1},{4,6},{5,7},{6,4},{7,5}} | collective-permute-start | bytes 196616 | tf_op jit(solution)/shard_map/ppermute | solution.py:535
  84.2 4.4 %collective-permute-start.11 = (bf16[16,2048]{1,0:T(8,128)(2,1)S(1)}, bf16[16,2048]{1,0:T(8,128)(2,1)S(1)}, u32[]{:S(2)}, u32[]{:S(2)}) collective-permute-start(bf16[16,2048]{1,0:T(8,128)(2,1)S(1)} %get-tuple-element.49), channel_id=1, source_target_pairs={{0,3},{1,2},{2,1},{3,0},{4,7},{5,6},{6,5},{7,4}} | collective-permute-start | bytes 196616 | tf_op jit(solution)/shard_map/ppermute | solution.py:535
  84.7 3.9 %copy-start.1 = (bf16[64,2048]{1,0:T(8,128)(2,1)S(1)}, bf16[64,2048]{1,0:T(8,128)(2,1)}, u32[]{:S(2)}) copy-start(bf16[64,2048]{1,0:T(8,128)(2,1)} %get-tuple-element.50.refs_4_) | copy-start | bytes 786436
where the time goes:
time: 114 us; the launch traced here: 113 us
  Pallas kernels  98.2 us (86%)
  starting transfers between devices  9.66 us (8%)
  local copies, waits for them, and re-layouts  3.51 us (3%)
  waiting for transfers between devices  1.17 us (1%)
    pallas_call x2, Pallas kernels, out_product(): pl.pallas_call(functools.partial(out_kernel, layer, fuse), out_shape=out_...  50.7 us
    pallas_call x2, Pallas kernels, attend(): pl.pallas_call(functools.partial(attend_kernel, layer, len(args)), out_sh...  20.6 us
    pallas_call x4, Pallas kernels, copy_cache(): pl.pallas_call(functools.partial(copy_kernel, layer, first, last, len(arg...  14 us
    pallas_call x1, Pallas kernels, first_qkv(): pl.pallas_call(first_qkv_kernel, out_shape=[sds((MINE, QW))] * 4 + [sds((...  12.9 us
    ppermute x12, starting transfers between devices, swap(): lax.ppermute(parts[i], 'model', [(m, m ^ i) for m in range(GROUPS)])  9.66 us
    unnamed x21, local copies, waits for them, and re-layouts  3.51 us
  transfers between devices with their start and end apart: 12, of which 3 were waited for; matrix products, arithmetic and copies ran while one was open for 0% of the time, Pallas kernels for 12%

commit v1 on v0

--- a/solution.py
+++ b/solution.py
@@ -23,7 +23,9 @@
 CH = 512
 NJ = QW // CH
 QKV = QW + 2 * HD
-WO_SLOTS = 6
+WO_SLOTS = 4
+AHEAD = 4
+Q_AHEAD = 6
 BLK = 256
 VM = pltpu.VMEM
 VSPEC = pl.BlockSpec(memory_space=pltpu.VMEM)
@@ -63,54 +65,125 @@
     return other
 
 
-def first_qkv_kernel(x, wq, wk, wv, q0, q1, q2, q3, k_new, v_new, buf, acc, xbuf, sems, x_sem):
+def first_qkv_kernel(x, wq, wk, wv, r0, r1, r2, r3, k_new, v_new,
+                     xbuf, wbuf, kvbuf, acc, qbuf, rbuf, x_sem, w_sems, kv_sems, ssems, rsems):
     me = lax.axis_index("model")
-    chunks = D // CH
+    depth = D // NJ
+
+    def cols(n):
+        return pl.ds(pl.multiple_of(n * CH, CH), CH)
+
+    def w_copy(step):
+        rows = pl.ds(pl.multiple_of(step % NJ * depth, depth), depth)
+        return pltpu.make_async_copy(wq.at[0, rows, cols(step // NJ)], wbuf.at[step], w_sems.at[step])
+
+    def send(i, n):
+        dev = xor_id(me, i)
+        rows = pl.ds(pl.multiple_of(dev * MINE, MINE), MINE)
+        return pltpu.make_async_remote_copy(
+            src_ref=qbuf.at[rows, cols(n)], dst_ref=rbuf.at[i - 1, :, cols(n)],
+            send_sem=ssems.at[i - 1, n], recv_sem=rsems.at[i - 1, n],
+            device_id={"model": dev}, device_id_type=pl.DeviceIdType.MESH)
+
     x_copy = pltpu.make_async_copy(x, xbuf, x_sem)
     x_copy.start()
-
-    def start(c, _):
-        for cp in qkv_copies(0, c, c, wq, wk, wv, buf, sems):
-            cp.start()
-        return 0
-
-    lax.fori_loop(0, chunks, start, 0)
-    acc[...] = jnp.zeros_like(acc)
+    kv_copies = [pltpu.make_async_copy(w.at[0], kvbuf.at[:, pl.ds(i * HD, HD)], kv_sems.at[i]) for i, w in enumerate((wk, wv))]
+
+    def start(step, _):
+        w_copy(step).start()
+        return 0
+
+    lax.fori_loop(0, AHEAD, start, 0)
+
+    barrier = pltpu.get_barrier_semaphore()
+    for i in range(1, GROUPS):
+        pl.semaphore_signal(barrier, inc=1, device_id={"model": xor_id(me, i)}, device_id_type=pl.DeviceIdType.MESH)
     x_copy.wait()
 
-    def step(c, _):
-        for cp in qkv_copies(0, c, c, wq, wk, wv, buf, sems):
-            cp.wait()
-        cols = pl.ds(pl.multiple_of(c * CH, CH), CH)
-        acc[...] += jnp.dot(xbuf[:, cols], buf[c], preferred_element_type=F32)
-        return 0
-
-    lax.fori_loop(0, chunks, step, 0)
-    write_qkv(me, acc, (q0, q1, q2, q3), k_new, v_new)
+    def group(n):
+        acc[...] = jnp.zeros_like(acc)
+
+        def step(k, _):
+            w_copy(n * NJ + k).wait()
+
+            @pl.when(n * NJ + k + AHEAD < NJ * NJ)
+            def _():
+                w_copy(n * NJ + k + AHEAD).start()
+            part = xbuf[:, pl.ds(pl.multiple_of(k * depth, depth), depth)]
+            acc[...] += jnp.dot(part, wbuf[n * NJ + k], preferred_element_type=F32)
+            return 0
+
+        lax.fori_loop(0, NJ, step, 0)
+        qbuf[:, cols(n)] = acc[...].astype(BF16)
+
+    def leave(n):
+        for i in (3, 2, 1):
+            send(i, n).start()
+
+    group(0)
+    pl.semaphore_wait(barrier, GROUPS - 1)
+    leave(0)
+
+    def later(n, _):
+        @pl.when(n == NJ - 1)
+        def _():
+            for cp in kv_copies:
+                cp.start()
+        group(n)
+        leave(n)
+        return 0
+
+    lax.fori_loop(1, NJ, later, 0)
+    mine = pl.ds(pl.multiple_of(me * MINE, MINE), MINE)
+    for cp in kv_copies:
+        cp.wait()
+    kv = jnp.zeros((MINE, 2 * HD), F32)
+    for k in range(NJ):
+        kv += jnp.dot(xbuf[mine, k * depth:(k + 1) * depth], kvbuf[k * depth:(k + 1) * depth, :], preferred_element_type=F32)
+    k_new[...] = kv[:, :HD].astype(BF16)
+    v_new[...] = kv[:, HD:].astype(BF16)
+    r0[...] = qbuf[mine, :]
+    for i, r in ((1, r1), (2, r2), (3, r3)):
+        for n in range(NJ):
+            send(i, n).wait_recv()
+        r[...] = rbuf[i - 1]
+
+    def drain(n, _):
+        for i in range(1, GROUPS):
+            send(i, n).wait_send()
+        return 0
+
+    lax.fori_loop(0, NJ, drain, 0)
 
 
 def first_qkv(x, wq, wk, wv):
-    n = D // CH
     return pl.pallas_call(
         first_qkv_kernel,
         out_shape=[sds((MINE, QW))] * 4 + [sds((MINE, HD))] * 2,
         in_specs=[ASPEC] * 4,
         out_specs=[VSPEC] * 6,
         scratch_shapes=[
-            VM((n, CH, QKV), BF16),
-            VM((ROWS, QKV), F32),
             VM((ROWS, D), BF16),
-            pltpu.SemaphoreType.DMA((3, n)),
+            VM((NJ * NJ, D // NJ, CH), BF16),
+            VM((D, 2 * HD), BF16),
+            VM((ROWS, CH), F32),
+            VM((ROWS, QW), BF16),
+            VM((GROUPS - 1, MINE, QW), BF16),
             pltpu.SemaphoreType.DMA,
+            pltpu.SemaphoreType.DMA((NJ * NJ,)),
+            pltpu.SemaphoreType.DMA((2,)),
+            pltpu.SemaphoreType.DMA((GROUPS - 1, NJ)),
+            pltpu.SemaphoreType.DMA((GROUPS - 1, NJ)),
         ],
-        compiler_params=pltpu.CompilerParams(vmem_limit_bytes=BIG),
+        compiler_params=pltpu.CompilerParams(vmem_limit_bytes=53 * MIB, collective_id=2, has_side_effects=True),
         cost_estimate=pl.CostEstimate(flops=2 * ROWS * D * QKV, bytes_accessed=2 * D * QKV, transcendentals=0),
         name="first_qkv",
     )(x, wq, wk, wv)
 
 
-K_CUT = 6
-V_CUT = 10
+K_CUT = (0, 6)
+V_CUT = (10, 10)
+READ_AHEAD = 2
 
 
 def put_row(buf, b, length, row):
@@ -135,15 +208,15 @@
         for n in range(self.count):
             self.take(n).start()
 
-    def forward(self):
+    def forward(self, n):
         me = lax.axis_index("model")
-        for n in range(self.count):
-            self.take(n).wait()
-            b = self.first + n
-            put_row(self.buf, n, self.lens[me * MINE + b], self.new[pl.ds(b, 1), :])
-            if n:
-                self.give(n - 1).start()
-        self.give(self.count - 1).start()
+        self.take(n).wait()
+        b = self.first + n
+        put_row(self.buf, n, self.lens[me * MINE + b], self.new[pl.ds(b, 1), :])
+        if n:
+            self.give(n - 1).start()
+        if n == self.count - 1:
+            self.give(n).start()
 
     def finish(self):
         for n in range(self.count):
@@ -159,7 +232,8 @@
     lens, new, src = refs[:3]
     share = Share(layer, first, last, lens, new, src, *refs[n_in:])
     share.start()
-    share.forward()
+    for n in range(share.count):
+        share.forward(n)
     share.finish()
 
 
@@ -184,13 +258,11 @@
 
 def attend_kernel(layer, n_in, *refs):
     lens, r0, r1, r2, r3, k_new, v_new, k_cache, v_cache = refs[:9]
-    c0, c1, c2, c3, k_out, v_out, kbuf, vbuf, qbuf, cbuf, new_kv, ksems, vsems = refs[n_in:n_in + 13]
-    shares = refs[n_in + 13:]
-    k_share = Share(layer, K_CUT, MINE, lens, k_new, k_cache, k_out, *shares[:3])
-    v_share = Share(layer, 0, V_CUT, lens, v_new, v_cache, v_out, *shares[3:])
+    c0, c1, c2, c3, k_out, v_out, kbuf, vbuf, qbuf, cbuf, new_kv, ksems, vsems, ko_sems, vo_sems = refs[n_in:]
     me = lax.axis_index("model")
     n_heads = GROUPS * LH
     scale = HD ** -0.5
+    caches = ((k_cache, kbuf, ksems, k_out, ko_sems, K_CUT[layer], MINE), (v_cache, vbuf, vsems, v_out, vo_sems, 0, V_CUT[layer]))
 
     def length(b):
         return lens[me * MINE + b]
@@ -198,45 +270,49 @@
     def tier_of(b, n):
         return jnp.logical_and(length(b) < TIERS[n], length(b) >= (TIERS[n - 1] if n else BLK))
 
-    def copies(b, part):
-        cut = pl.ds(*part)
-        return (pltpu.make_async_copy(k_cache.at[layer, b, cut, :], kbuf.at[b, cut, :], ksems.at[b, part[0] // BLK]),
-                pltpu.make_async_copy(v_cache.at[layer, b, cut, :], vbuf.at[b, cut, :], vsems.at[b, part[0] // BLK]))
-
-    def start_first(b, _):
-        for cp in copies(b, (0, BLK)):
-            cp.start()
-        return 0
-
-    def start_rest(b, _):
-        for n, size in enumerate(TIERS):
-            @pl.when(tier_of(b, n))
-            def _(size=size):
-                for cp in copies(b, (BLK, size - BLK)):
-                    cp.start()
-        return 0
-
-    lax.fori_loop(0, MINE, start_first, 0)
-    lax.fori_loop(0, MINE, start_rest, 0)
-    k_share.start()
-    v_share.start()
-
+    def reads(b, act):
+        for cache, buf, sems, _, _, first, last in caches:
+            def part(start, size, cache=cache, buf=buf, sems=sems):
+                cut = pl.ds(start, size)
+                return pltpu.make_async_copy(cache.at[layer, b, cut, :], buf.at[b, cut, :], sems.at[b, min(start, 1)])
+
+            @pl.when(jnp.logical_and(b >= first, b < last))
+            def _(part=part):
+                act(part(0, SEQ))
+
+            @pl.when(jnp.logical_or(b < first, b >= last))
+            def _(part=part):
+                act(part(0, BLK))
+                for n, size in enumerate(TIERS):
+                    @pl.when(tier_of(b, n))
+                    def _(size=size):
+                        act(part(BLK, size - BLK))
+
+    def writes(b, act):
+        for _, buf, _, out, sems, first, last in caches:
+            @pl.when(jnp.logical_and(b >= first, b < last))
+            def _(buf=buf, out=out, sems=sems):
+                act(pltpu.make_async_copy(buf.at[b], out.at[layer, b], sems.at[b]))
+
+    def each(g, do):
+        for i in range(GRP):
+            do(g * GRP + i)
+
+    def start_group(g, _):
+        each(g, lambda b: reads(b, lambda cp: cp.start()))
+        return 0
+
+    lax.fori_loop(0, READ_AHEAD, start_group, 0)
     for i, r in enumerate((r0, r1, r2, r3)):
         qbuf[:, i * LH:(i + 1) * LH, :] = r[...].reshape(MINE, LH, HD)
-
     for b in range(MINE):
         new_kv[0, b] = k_new[b:b + 1, :].astype(F32)
         new_kv[1, b] = v_new[b:b + 1, :].astype(F32)
 
-    def new_rows(b):
-        put_row(kbuf, b, length(b), new_kv[0, b].astype(BF16))
-        put_row(vbuf, b, length(b), new_kv[1, b].astype(BF16))
-
     def context(seqs, size):
         scores = []
         for b in seqs:
-            s = lax.dot_general(qbuf[b], kbuf[b, 0:size, :], (((1,), (1,)), ((), ())),
-                                preferred_element_type=F32)
+            s = lax.dot_general(qbuf[b], kbuf[b, 0:size, :], (((1,), (1,)), ((), ())), preferred_element_type=F32)
             pos = lax.broadcasted_iota(jnp.int32, (n_heads, size), 1)
             scores.append(jnp.where(pos <= length(b), s * scale, -jnp.inf))
         expos = [jnp.exp(s - jnp.max(s, axis=1, keepdims=True)) for s in scores]
@@ -244,48 +320,48 @@
         for b, p in zip(seqs, probs):
             cbuf[b] = jnp.dot(p, vbuf[b, 0:size, :], preferred_element_type=F32).astype(BF16)
 
-    def first_blocks(g, _):
-        seqs = [g * GRP + i for i in range(GRP)]
-        for b in seqs:
-            for cp in copies(b, (0, BLK)):
-                cp.wait()
-
-            @pl.when(length(b) < BLK)
-            def _(b=b):
-                new_rows(b)
-        context(seqs, BLK)
-        return 0
-
-    lax.fori_loop(0, MINE // GRP, first_blocks, 0)
-    k_share.forward()
-    v_share.forward()
-
-    def rest(b, _):
+    def ready(b):
+        reads(b, lambda cp: cp.wait())
+        put_row(kbuf, b, length(b), new_kv[0, b].astype(BF16))
+        put_row(vbuf, b, length(b), new_kv[1, b].astype(BF16))
+
+    def long_one(b, _):
         for n, size in enumerate(TIERS):
             @pl.when(tier_of(b, n))
             def _(size=size):
-                for cp in copies(b, (BLK, size - BLK)):
-                    cp.wait()
-                new_rows(b)
                 context((b,), size)
         return 0
 
-    lax.fori_loop(0, MINE, rest, 0)
-
+    def group(g, _):
+        each(g, ready)
+
+        @pl.when(g + READ_AHEAD < MINE // GRP)
+        def _():
+            start_group(g + READ_AHEAD, 0)
+        context([g * GRP + i for i in range(GRP)], BLK)
+        each(g, lambda b: writes(b, lambda cp: cp.start()))
+        lax.fori_loop(g * GRP, (g + 1) * GRP, long_one, 0)
+        return 0
+
+    lax.fori_loop(0, MINE // GRP, group, 0)
     for i, c in enumerate((c0, c1, c2, c3)):
         c[...] = cbuf[:, i * LH:(i + 1) * LH, :].reshape(MINE, QW)
-    k_share.finish()
-    v_share.finish()
-
-
-def attend(layer, lens, rs, k_new, v_new, k_cache, v_cache, k_out, v_out):
-    args = [lens, *rs, k_new, v_new, k_cache, v_cache, k_out] + ([v_out] if v_out is not None else [])
+
+    def finish(b, _):
+        writes(b, lambda cp: cp.wait())
+        return 0
+
+    lax.fori_loop(0, MINE, finish, 0)
+
+
+def attend(layer, lens, rs, k_new, v_new, k_cache, v_cache, priors):
+    args = [lens, *rs, k_new, v_new, k_cache, v_cache, *priors]
     return pl.pallas_call(
         functools.partial(attend_kernel, layer, len(args)),
         out_shape=[sds((MINE, QW))] * 4 + [sds(k_cache.shape)] * 2,
         in_specs=[SSPEC] + [VSPEC] * 6 + [ASPEC] * (len(args) - 7),
         out_specs=[VSPEC] * 4 + [ASPEC] * 2,
-        input_output_aliases={9: 4} if v_out is None else {9: 4, 10: 5},
+        input_output_aliases={9: 4, 10: 5} if priors else {},
         scratch_shapes=[
             VM((MINE, SEQ, HD), BF16),
             VM((MINE, SEQ, HD), BF16),
@@ -294,8 +370,8 @@
             VM((2, MINE, 1, HD), F32),
             pltpu.SemaphoreType.DMA((MINE, 2)),
             pltpu.SemaphoreType.DMA((MINE, 2)),
-            *Share.scratch(K_CUT, MINE),
-            *Share.scratch(0, V_CUT),
+            pltpu.SemaphoreType.DMA((MINE,)),
+            pltpu.SemaphoreType.DMA((MINE,)),
         ],
         compiler_params=pltpu.CompilerParams(vmem_limit_bytes=BIG),
         cost_estimate=pl.CostEstimate(flops=5_000_000_000, bytes_accessed=8 * MIB, transcendentals=0),
@@ -327,8 +403,15 @@
         slot = step % WO_SLOTS
         return pltpu.make_async_copy(wo.at[layer, :, cols(chunk)], wbuf.at[slot], w_sems.at[slot])
 
-    def q_copies(chunk, slot):
+    def q_copies(slot):
+        chip_of = lax.rem(lax.div(me, 2) + slot // (2 * NJ), 2)
+        core_of = lax.rem(lax.rem(me, 2) + slot % 2, 2)
+        chunk = (chip_of * 2 + core_of) * NJ + slot % (2 * NJ) // 2
         return qkv_copies(layer + 1, chunk, slot, wq, wk, wv, qbuf, q_sems)
+
+    def start_q(slot):
+        for cp in q_copies(slot):
+            cp.start()
 
     def send(kind, j, src, dst, dev):
         return pltpu.make_async_remote_copy(
@@ -352,7 +435,7 @@
         wo_copy(step).start()
         return 0
 
-    lax.fori_loop(0, WO_SLOTS, start_wo, 0)
+    lax.fori_loop(0, WO_SLOTS - 1, start_wo, 0)
     if fuse:
         res_copy = pltpu.make_async_copy(
             res.at[:, pl.ds(pl.multiple_of(me * QW, QW), QW)], resv, res_sem)
@@ -368,16 +451,13 @@
     barrier = pltpu.get_barrier_semaphore()
     for dev in (partner, cross):
         pl.semaphore_signal(barrier, inc=1, device_id={"model": dev}, device_id_type=pl.DeviceIdType.MESH)
-    pl.semaphore_wait(barrier, 2)
-
     def part_sum(step):
         wo_copy(step).wait()
+
+        @pl.when(step + WO_SLOTS - 1 < 4 * NJ)
+        def _():
+            wo_copy(step + WO_SLOTS - 1).start()
         return jnp.dot(ctx[...], wbuf[step % WO_SLOTS], preferred_element_type=F32)
-
-    def refill(step):
-        @pl.when(step + WO_SLOTS < 4 * NJ)
-        def _():
-            wo_copy(step + WO_SLOTS).start()
 
     def send_across(j):
         pair_a(j).wait_recv()
@@ -386,14 +466,16 @@
 
     def phase_a(j, _):
         send_a[j] = part_sum(2 * j)
+
+        @pl.when(j == 0)
+        def _():
+            pl.semaphore_wait(barrier, 2)
         pair_a(j).start()
-        refill(2 * j)
 
         @pl.when(j > 0)
         def _():
             send_across(j - 1)
         send_c[j] = part_sum(2 * j + 1)
-        refill(2 * j + 1)
         return 0
 
     lax.fori_loop(0, NJ, phase_a, 0)
@@ -403,31 +485,31 @@
         step = 2 * NJ + 2 * j
         send_b[j] = part_sum(step)
         pair_b(j).start()
-        refill(step)
         own[j] = part_sum(step + 1)
-        refill(step + 1)
         if fuse:
-            for i, owner in enumerate((me, partner)):
-                for cp in q_copies(owner * NJ + j, 2 * j + i):
-                    cp.start()
+            @pl.when(j >= NJ - 2)
+            def _():
+                start_q(2 * (j - NJ + 2))
+                start_q(2 * (j - NJ + 2) + 1)
+
+            @pl.when(j == NJ - 1)
+            def _():
+                start_q(4)
+                start_q(5)
         return 0
 
     lax.fori_loop(0, NJ, phase_b, 0)
-    if fuse:
-        def start_far(j, _):
-            for i, owner in enumerate((cross, diag)):
-                for cp in q_copies(owner * NJ + j, 2 * NJ + 2 * j + i):
-                    cp.start()
-            return 0
-
-        lax.fori_loop(0, NJ, start_far, 0)
     res_copy.wait()
 
     def next_q(owner, j, slot):
         if fuse:
             chunk = owner * NJ + j
-            for cp in q_copies(chunk, slot):
+            for cp in q_copies(slot):
                 cp.wait()
+
+            @pl.when(slot + Q_AHEAD < 4 * NJ)
+            def _():
+                start_q(slot + Q_AHEAD)
             acc[...] += jnp.dot(hid[:, cols(chunk)], qbuf[slot], preferred_element_type=F32)
 
     def from_partner(j):
@@ -523,7 +605,7 @@
         out_specs=out_specs,
         scratch_shapes=extra + shared,
         compiler_params=pltpu.CompilerParams(
-            vmem_limit_bytes=58 * MIB if fuse else 32 * MIB, collective_id=layer, has_side_effects=True),
+            vmem_limit_bytes=53 * MIB if fuse else 32 * MIB, collective_id=layer, has_side_effects=True),
         cost_estimate=pl.CostEstimate(flops=flops, bytes_accessed=flops // ROWS, transcendentals=0),
         name=f"out_product_{layer}",
     )(*args)
@@ -540,17 +622,18 @@
     cache_spec = P(None, ("replica", "model"), None, None)
 
     def device_step(x, cache_len, w_query, w_key, w_value, w_out, k_cache, v_cache):
-        *qs, k_new, v_new = first_qkv(x, w_query, w_key, w_value)
-        k_out = v_out = None
-        res = x
+        *rs, k_new, v_new = first_qkv(x, w_query, w_key, w_value)
+        priors = ()
         for layer in range(2):
-            rs = swap(qs)
-            k_out = copy_cache(layer, 0, K_CUT, cache_len, k_new, k_cache, k_out)
-            *cs, k_out, v_out = attend(layer, cache_len, rs, k_new, v_new, k_cache, v_cache, k_out, v_out)
+            if layer:
+                k_out = copy_cache(layer, 0, K_CUT[layer], cache_len, k_new, k_cache, k_out)
+                priors = (k_out, v_out)
+            *cs, k_out, v_out = attend(layer, cache_len, rs, k_new, v_new, k_cache, v_cache, priors)
             ds = swap(cs)
-            v_out = copy_cache(layer, V_CUT, MINE, cache_len, v_new, v_cache, v_out)
+            v_out = copy_cache(layer, V_CUT[layer], MINE, cache_len, v_new, v_cache, v_out)
             if layer == 0:
                 *qs, k_new, v_new, res = out_product(0, True, ds, x, w_out, (w_query, w_key, w_value))
+                rs = swap(qs)
             else:
                 out = out_product(1, False, ds, res, w_out, ())
         return out, k_out, v_out

time: 114 us -> 107 us (0.939)
  starting transfers between devices: 9.66 us -> 5.62 us
  local copies, waits for them, and re-layouts: 3.51 us -> 0.98 us
  Pallas kernels: 98.2 us -> 99.5 us
    pallas_call x1, Pallas kernels: 12.9 us -> 17.6 us  [first_qkv(): pl.pallas_call(first_qkv_kernel, out_shape=[sds((MINE, QW))] * 4 + [sds((...]
    ppermute x12 -> x9, starting transfers between devices: 9.66 us -> 5.62 us  [swap(): lax.ppermute(parts[i], 'model', [(m, m ^ i) for m in range(GROUPS)])]
    pallas_call x4 -> x3, Pallas kernels: 14 us -> 10.5 us  [copy_cache(): pl.pallas_call(functools.partial(copy_kernel, layer, first, last, len(arg...]
    unnamed x21 -> x3, local copies, waits for them, and re-layouts: 3.51 us -> 0.98 us
    pallas_call x2, Pallas kernels: 20.6 us -> 22.9 us  [attend(): pl.pallas_call(functools.partial(attend_kernel, layer, len(args)), out_sh...]
    pallas_call x2, Pallas kernels: 50.7 us -> 48.6 us  [out_product(): pl.pallas_call(functools.partial(out_kernel, layer, fuse), out_shape=out_...]
  transfers between devices with their start and end apart: 12 -> 9, of which waited for: 3 -> 2; matrix products, arithmetic and copies ran while one was open for 0% -> 0% of each run, Pallas kernels for 12% -> 10%
where the time goes in v1:
time: 107 us
  Pallas kernels  99.5 us (93%)
  starting transfers between devices  5.62 us (5%)
    pallas_call x2, Pallas kernels, out_product(): pl.pallas_call(functools.partial(out_kernel, layer, fuse), out_shape=out_...  48.6 us
    pallas_call x2, Pallas kernels, attend(): pl.pallas_call(functools.partial(attend_kernel, layer, len(args)), out_sh...  22.9 us
    pallas_call x1, Pallas kernels, first_qkv(): pl.pallas_call(first_qkv_kernel, out_shape=[sds((MINE, QW))] * 4 + [sds((...  17.6 us
    pallas_call x3, Pallas kernels, copy_cache(): pl.pallas_call(functools.partial(copy_kernel, layer, first, last, len(arg...  10.5 us
    ppermute x9, starting transfers between devices, swap(): lax.ppermute(parts[i], 'model', [(m, m ^ i) for m in range(GROUPS)])  5.62 us
  transfers between devices with their start and end apart: 9, of which 2 were waited for; matrix products, arithmetic and copies ran while one was open for 0% of the time, Pallas kernels for 10%

profile of v1, /device:TPU:0, one launch (start us, length us, event | category | flops | bytes accessed | tf_op | source)
XLA Modules:
  0.0 107.3 jit_solution(10369395068105155556)
XLA Ops:
  0.6 17.6 %first_qkv.1 = (bf16[16,2048]{1,0:T(8,128)(2,1)S(1)}, bf16[16,2048]{1,0:T(8,128)(2,1)S(1)}, bf16[16,2048]{1,0:T(8,128)(2,1)S(1)}, bf16[16,2048]{1,0:T(8,128)(2,1...) custom-call(bf16[64,8192]{1,0:T(8,128)(2,1)} %refs_4_.1, bf16[2,8192,2048]{2,1,0:T(8,128)(2,1)} %refs_6_.1, ...), custom_call_target="tpu_custom_call" | custom-call | flops 2415919104 | bytes 37748736 | tf_op jit(solution)/shard_map/first_qkv/pallas_call | solution.py:160
  18.2 12.5 %attend_0.1 = (bf16[16,2048]{1,0:T(8,128)(2,1)S(1)}, bf16[16,2048]{1,0:T(8,128)(2,1)S(1)}, bf16[16,2048]{1,0:T(8,128)(2,1)S(1)}, bf16[16,2048]{1,0:T(8,128)(2,1)...) custom-call(s32[64]{0:T(128)S(1)} %copy-done, ...), custom_call_target="tpu_custom_call" | custom-call | flops 5000000000 | bytes 8388608 | tf_op jit(solution)/shard_map/attend_0/pallas_call | solution.py:359
  30.8 0.0 collective-permute-start
  30.8 0.0 collective-permute-start.1
  30.8 1.8 %collective-permute-start.2 = (bf16[16,2048]{1,0:T(8,128)(2,1)S(1)}, bf16[16,2048]{1,0:T(8,128)(2,1)S(1)}, u32[]{:S(2)}, u32[]{:S(2)}) collective-permute-start(bf16[16,2048]{1,0:T(8,128)(2,1)S(1)} %get-tuple-element.37), channel_id=1, source_target_pairs={{0,3},{1,2},{2,1},{3,0},{4,7},{5,6},{6,5},{7,4}} | collective-permute-start | bytes 196616 | tf_op jit(solution)/shard_map/ppermute | solution.py:617
  32.6 3.5 %copy_cache_0.1.refs_10_ = bf16[2,16,2048,128]{3,2,1,0:T(8,128)(2,1)} custom-call(s32[64]{0:T(128)S(1)} %copy-done, bf16[16,128]{1,0:T(8,128)(2,1)S(1)} %get-tuple-element.33.refs_6_.refs_1_, bf16[2,16,2048,128]{3,2,1,0:T(8,128)(2,1)} %refs_2_.5, bf16[2,16,2048,128]{3,2,1,0:T(8,128)(2,1)} %get-tuple-element.45.refs_3_), custom_call_target="tpu_custom_call", output_to_operand_aliasing={{}: (3, {})} | custom-call | flops 5000000000 | bytes 16777216 | tf_op jit(solution)/shard_map/copy_cache_0/pallas_call | solution.py:242
  36.1 0.0 collective-permute-done.refs_1_
  36.2 0.0 collective-permute-done.1.refs_2_
  36.2 0.0 collective-permute-done.2.refs_3_
  36.2 24.8 %out_product_0.1 = (bf16[16,2048]{1,0:T(8,128)(2,1)S(1)}, bf16[16,2048]{1,0:T(8,128)(2,1)S(1)}, bf16[16,2048]{1,0:T(8,128)(2,1)S(1)}, bf16[16,2048]{1,0:T(8,128)...) custom-call(bf16[16,2048]{1,0:T(8,128)(2,1)S(1)} %get-tuple-element.34.refs_0_, ...), custom_call_target="tpu_custom_call" | custom-call | flops 4563402752 | bytes 71303168 | tf_op jit(solution)/shard_map/out_product_0/pallas_call | solution.py:601
  61.0 0.2 collective-permute-start.3
  61.1 1.4 %collective-permute-start.4 = (bf16[16,2048]{1,0:T(8,128)(2,1)S(1)}, bf16[16,2048]{1,0:T(8,128)(2,1)S(1)}, u32[]{:S(2)}, u32[]{:S(2)}) collective-permute-start(bf16[16,2048]{1,0:T(8,128)(2,1)S(1)} %get-tuple-element.40), channel_id=1, source_target_pairs={{0,2},{1,3},{2,0},{3,1},{4,6},{5,7},{6,4},{7,5}} | collective-permute-start | bytes 196616 | tf_op jit(solution)/shard_map/ppermute | solution.py:617
  62.5 0.3 collective-permute-start.5
  62.9 3.5 %copy_cache_1.2.refs_9_ = bf16[2,16,2048,128]{3,2,1,0:T(8,128)(2,1)} custom-call(s32[64]{0:T(128)S(1)} %copy-done, bf16[16,128]{1,0:T(8,128)(2,1)S(1)} %get-tuple-element.42.refs_1_.refs_5_, bf16[2,16,2048,128]{3,2,1,0:T(8,128)(2,1)} %refs_7_.5, bf16[2,16,2048,128]{3,2,1,0:T(8,128)(2,1)} %get-tuple-element.44.refs_3_), custom_call_target="tpu_custom_call", output_to_operand_aliasing={{}: (3, {})} | custom-call | flops 5000000000 | bytes 16777216 | tf_op jit(solution)/shard_map/copy_cache_1/pallas_call | solution.py:242
  66.4 0.0 collective-permute-done.3.refs_2_
  66.4 0.3 collective-permute-done.5.refs_4_
  66.6 10.3 %attend_1.1 = (bf16[16,2048]{1,0:T(8,128)(2,1)S(1)}, bf16[16,2048]{1,0:T(8,128)(2,1)S(1)}, bf16[16,2048]{1,0:T(8,128)(2,1)S(1)}, bf16[16,2048]{1,0:T(8,128)(2,1)...) custom-call(s32[64]{0:T(128)S(1)} %copy-done, ...), custom_call_target="tpu_custom_call", output_to_operand_aliasing={{4}: (9, {}), {5}: (10, {})} | custom-call | flops 5000000000 | bytes 8388608 | tf_op jit(solution)/shard_map/attend_1/pallas_call | solution.py:359
  77.0 0.0 collective-permute-start.6
  77.0 1.1 collective-permute-start.7
  78.1 0.8 collective-permute-start.8
  78.9 3.5 %copy_cache_1.3 = bf16[2,16,2048,128]{3,2,1,0:T(8,128)(2,1)} custom-call(s32[64]{0:T(128)S(1)} %copy-done, bf16[16,128]{1,0:T(8,128)(2,1)S(1)} %get-tuple-element.43.refs_6_.refs_1_, bf16[2,16,2048,128]{3,2,1,0:T(8,128)(2,1)} %refs_2_.5, bf16[2,16,2048,128]{3,2,1,0:T(8,128)(2,1)} %get-tuple-element.52.refs_3_), custom_call_target="tpu_custom_call", output_to_operand_aliasing={{}: (3, {})} | custom-call | flops 5000000000 | bytes 16777216 | tf_op jit(solution)/shard_map/copy_cache_1/pallas_call | solution.py:242
  82.4 0.1 collective-permute-done.8.refs_3_
  82.5 23.8 %out_product_1.1 = bf16[64,8192]{1,0:T(8,128)(2,1)S(1)} custom-call(bf16[16,2048]{1,0:T(8,128)(2,1)S(1)} %get-tuple-element.46.refs_0_, bf16[16,2048]{1,0:T(8,128)(2,1)S(1)} %collective-permute-done.6.refs_1_, bf16[16,2048]{1,0:T(8,128)(2,1)S(1)} %collective-permute-done.7.refs_2_, bf16[16,2048]{1,0:T(8,128)(2,1)S(1)} %collective-permute-done.8.refs_3_, ...), custom_call_target="tpu_custom_call" | custom-call | flops 2147483648 | bytes 33554432 | tf_op jit(solution)/shard_map/out_product_1/pallas_call | solution.py:601
  106.3 1.0 copy.22
  (5 shorter events, 0.0 us)
Async XLA Ops:
  0.6 17.6 %copy-start = (s32[64]{0:T(128)S(1)}, s32[64]{0:T(128)}, u32[]{:S(2)}) copy-start(s32[64]{0:T(128)} %refs_0_.9) | copy-start | bytes 772
  30.8 5.4 %collective-permute-start = (bf16[16,2048]{1,0:T(8,128)(2,1)S(1)}, bf16[16,2048]{1,0:T(8,128)(2,1)S(1)}, u32[]{:S(2)}, u32[]{:S(2)}) collective-permute-start(bf16[16,2048]{1,0:T(8,128)(2,1)S(1)} %get-tuple-element.35), channel_id=1, source_target_pairs={{0,1},{1,0},{2,3},{3,2},{4,5},{5,4},{6,7},{7,6}} | collective-permute-start | bytes 196616 | tf_op jit(solution)/shard_map/ppermute | solution.py:617
  30.8 5.4 %collective-permute-start.1 = (bf16[16,2048]{1,0:T(8,128)(2,1)S(1)}, bf16[16,2048]{1,0:T(8,128)(2,1)S(1)}, u32[]{:S(2)}, u32[]{:S(2)}) collective-permute-start(bf16[16,2048]{1,0:T(8,128)(2,1)S(1)} %get-tuple-element.36), channel_id=1, source_target_pairs={{0,2},{1,3},{2,0},{3,1},{4,6},{5,7},{6,4},{7,5}} | collective-permute-start | bytes 196616 | tf_op jit(solution)/shard_map/ppermute | solution.py:617
  30.8 5.4 %collective-permute-start.2 = (bf16[16,2048]{1,0:T(8,128)(2,1)S(1)}, bf16[16,2048]{1,0:T(8,128)(2,1)S(1)}, u32[]{:S(2)}, u32[]{:S(2)}) collective-permute-start(bf16[16,2048]{1,0:T(8,128)(2,1)S(1)} %get-tuple-element.37), channel_id=1, source_target_pairs={{0,3},{1,2},{2,1},{3,0},{4,7},{5,6},{6,5},{7,4}} | collective-permute-start | bytes 196616 | tf_op jit(solution)/shard_map/ppermute | solution.py:617
  61.0 5.4 %collective-permute-start.3 = (bf16[16,2048]{1,0:T(8,128)(2,1)S(1)}, bf16[16,2048]{1,0:T(8,128)(2,1)S(1)}, u32[]{:S(2)}, u32[]{:S(2)}) collective-permute-start(bf16[16,2048]{1,0:T(8,128)(2,1)S(1)} %get-tuple-element.39), channel_id=1, source_target_pairs={{0,1},{1,0},{2,3},{3,2},{4,5},{5,4},{6,7},{7,6}} | collective-permute-start | bytes 196616 | tf_op jit(solution)/shard_map/ppermute | solution.py:617
  61.1 5.2 %collective-permute-start.4 = (bf16[16,2048]{1,0:T(8,128)(2,1)S(1)}, bf16[16,2048]{1,0:T(8,128)(2,1)S(1)}, u32[]{:S(2)}, u32[]{:S(2)}) collective-permute-start(bf16[16,2048]{1,0:T(8,128)(2,1)S(1)} %get-tuple-element.40), channel_id=1, source_target_pairs={{0,2},{1,3},{2,0},{3,1},{4,6},{5,7},{6,4},{7,5}} | collective-permute-start | bytes 196616 | tf_op jit(solution)/shard_map/ppermute | solution.py:617
  62.5 4.1 %collective-permute-start.5 = (bf16[16,2048]{1,0:T(8,128)(2,1)S(1)}, bf16[16,2048]{1,0:T(8,128)(2,1)S(1)}, u32[]{:S(2)}, u32[]{:S(2)}) collective-permute-start(bf16[16,2048]{1,0:T(8,128)(2,1)S(1)} %get-tuple-element.41), channel_id=1, source_target_pairs={{0,3},{1,2},{2,1},{3,0},{4,7},{5,6},{6,5},{7,4}} | collective-permute-start | bytes 196616 | tf_op jit(solution)/shard_map/ppermute | solution.py:617
  77.0 5.4 %collective-permute-start.6 = (bf16[16,2048]{1,0:T(8,128)(2,1)S(1)}, bf16[16,2048]{1,0:T(8,128)(2,1)S(1)}, u32[]{:S(2)}, u32[]{:S(2)}) collective-permute-start(bf16[16,2048]{1,0:T(8,128)(2,1)S(1)} %get-tuple-element.47), channel_id=1, source_target_pairs={{0,1},{1,0},{2,3},{3,2},{4,5},{5,4},{6,7},{7,6}} | collective-permute-start | bytes 196616 | tf_op jit(solution)/shard_map/ppermute | solution.py:617
  77.0 5.4 %collective-permute-start.7 = (bf16[16,2048]{1,0:T(8,128)(2,1)S(1)}, bf16[16,2048]{1,0:T(8,128)(2,1)S(1)}, u32[]{:S(2)}, u32[]{:S(2)}) collective-permute-start(bf16[16,2048]{1,0:T(8,128)(2,1)S(1)} %get-tuple-element.48), channel_id=1, source_target_pairs={{0,2},{1,3},{2,0},{3,1},{4,6},{5,7},{6,4},{7,5}} | collective-permute-start | bytes 196616 | tf_op jit(solution)/shard_map/ppermute | solution.py:617
  78.1 4.4 %collective-permute-start.8 = (bf16[16,2048]{1,0:T(8,128)(2,1)S(1)}, bf16[16,2048]{1,0:T(8,128)(2,1)S(1)}, u32[]{:S(2)}, u32[]{:S(2)}) collective-permute-start(bf16[16,2048]{1,0:T(8,128)(2,1)S(1)} %get-tuple-element.49), channel_id=1, source_target_pairs={{0,3},{1,2},{2,1},{3,0},{4,7},{5,6},{6,5},{7,4}} | collective-permute-start | bytes 196616 | tf_op jit(solution)/shard_map/ppermute | solution.py:617

commit v2 on v1

--- a/solution.py
+++ b/solution.py
@@ -23,9 +23,10 @@
 CH = 512
 NJ = QW // CH
 QKV = QW + 2 * HD
-WO_SLOTS = 4
+WO_SLOTS = (8, 16)
+Q_SLOTS = 12
 AHEAD = 4
-Q_AHEAD = 6
+Q_FIRST = 4
 BLK = 256
 VM = pltpu.VMEM
 VSPEC = pl.BlockSpec(memory_space=pltpu.VMEM)
@@ -182,7 +183,7 @@
 
 
 K_CUT = (0, 6)
-V_CUT = (10, 10)
+V_CUT = (16, 16)
 READ_AHEAD = 2
 
 
@@ -252,7 +253,7 @@
     )(*args)
 
 
-GRP = 4
+GRP = 8
 TIERS = (512, 1024, 2048)
 
 
@@ -380,7 +381,7 @@
 
 
 def out_kernel(layer, fuse, *refs):
-    d_refs, (res, wo), refs = refs[:4], refs[4:6], refs[6:]
+    c_refs, (res, wo), refs = refs[:4], refs[4:6], refs[6:]
     if fuse:
         (wq, wk, wv), outs, refs = refs[:3], refs[3:10], refs[10:]
         q_outs, (k_new, v_new, res_out) = outs[:4], outs[4:]
@@ -391,6 +392,7 @@
     ctx, resv, wbuf, send_a, recv_a, send_c, recv_c, send_b, recv_b, own, w_sems, res_sem, ssems, rsems = refs
 
     me = lax.axis_index("model")
+    n_wo = WO_SLOTS[layer]
     partner, cross, diag = xor_id(me, 1), xor_id(me, 2), xor_id(me, 3)
 
     def cols(chunk):
@@ -400,14 +402,14 @@
         chip_of = lax.rem(lax.div(me, 2) + 1 - step // (2 * NJ), 2)
         core_of = lax.rem(lax.rem(me, 2) + 1 - step % 2, 2)
         chunk = (chip_of * 2 + core_of) * NJ + step % (2 * NJ) // 2
-        slot = step % WO_SLOTS
+        slot = step % n_wo
         return pltpu.make_async_copy(wo.at[layer, :, cols(chunk)], wbuf.at[slot], w_sems.at[slot])
 
     def q_copies(slot):
         chip_of = lax.rem(lax.div(me, 2) + slot // (2 * NJ), 2)
         core_of = lax.rem(lax.rem(me, 2) + slot % 2, 2)
         chunk = (chip_of * 2 + core_of) * NJ + slot % (2 * NJ) // 2
-        return qkv_copies(layer + 1, chunk, slot, wq, wk, wv, qbuf, q_sems)
+        return qkv_copies(layer + 1, chunk, slot % Q_SLOTS, wq, wk, wv, qbuf, q_sems)
 
     def start_q(slot):
         for cp in q_copies(slot):
@@ -418,14 +420,29 @@
             src_ref=src, dst_ref=dst, send_sem=ssems.at[kind, j], recv_sem=rsems.at[kind, j],
             device_id={"model": dev}, device_id_type=pl.DeviceIdType.MESH)
 
-    def pair_a(j):
-        return send(0, j, send_a.at[j], recv_a.at[j], partner)
+    half = ROWS // 2
+
+    def rows_of(h):
+        return pl.ds(pl.multiple_of(lax.rem(lax.div(me, 2) + h, 2) * half, half), half)
+
+    def context(i):
+        there = ctx.at[pl.ds(pl.multiple_of(me * MINE, MINE), MINE), :]
+        return send(6, i, c_refs[i], there, xor_id(me, i))
+
+    def pair_a(t):
+        part = (t % NJ, rows_of(t // NJ))
+        return send(0, t, send_a.at[part], recv_a.at[part], partner)
 
     def pair_b(j):
         return send(1, j, send_b.at[j], recv_b.at[j], partner)
 
-    def across(j):
-        return send(2, j, send_c.at[j], recv_c.at[j], cross)
+    def across(t):
+        part = (t % NJ, rows_of(t // NJ))
+        return send(2, t, send_c.at[part], recv_c.at[part], cross)
+
+    def across_here(t):
+        part = (t % NJ, rows_of(1 - t // NJ))
+        return send(2, t, send_c.at[part], recv_c.at[part], cross)
 
     def hidden(kind, j, owner, dev):
         part = hid.at[:, cols(owner * NJ + j)]
@@ -435,7 +452,7 @@
         wo_copy(step).start()
         return 0
 
-    lax.fori_loop(0, WO_SLOTS - 1, start_wo, 0)
+    lax.fori_loop(0, n_wo, start_wo, 0)
     if fuse:
         res_copy = pltpu.make_async_copy(
             res.at[:, pl.ds(pl.multiple_of(me * QW, QW), QW)], resv, res_sem)
@@ -443,59 +460,79 @@
         res_copy = pltpu.make_async_copy(res, resv, res_sem)
     res_copy.start()
 
-    for i, d in enumerate(d_refs):
-        ctx[pl.ds(pl.multiple_of(xor_id(me, i) * MINE, MINE), MINE), :] = d[...]
+    ctx[pl.ds(pl.multiple_of(me * MINE, MINE), MINE), :] = c_refs[0][...]
     if fuse:
         acc[...] = jnp.zeros_like(acc)
+        for slot in range(Q_FIRST):
+            start_q(slot)
 
     barrier = pltpu.get_barrier_semaphore()
-    for dev in (partner, cross):
-        pl.semaphore_signal(barrier, inc=1, device_id={"model": dev}, device_id_type=pl.DeviceIdType.MESH)
+    for i in range(1, GROUPS):
+        pl.semaphore_signal(barrier, inc=1, device_id={"model": xor_id(me, i)}, device_id_type=pl.DeviceIdType.MESH)
+    pl.semaphore_wait(barrier, GROUPS - 1)
+    for i in (1, 2, 3):
+        context(i).start()
+
     def part_sum(step):
         wo_copy(step).wait()
-
-        @pl.when(step + WO_SLOTS - 1 < 4 * NJ)
-        def _():
-            wo_copy(step + WO_SLOTS - 1).start()
-        return jnp.dot(ctx[...], wbuf[step % WO_SLOTS], preferred_element_type=F32)
-
-    def send_across(j):
-        pair_a(j).wait_recv()
-        send_c[j] += recv_a[j]
-        across(j).start()
-
-    def phase_a(j, _):
-        send_a[j] = part_sum(2 * j)
-
-        @pl.when(j == 0)
-        def _():
-            pl.semaphore_wait(barrier, 2)
-        pair_a(j).start()
-
-        @pl.when(j > 0)
-        def _():
-            send_across(j - 1)
-        send_c[j] = part_sum(2 * j + 1)
-        return 0
-
-    lax.fori_loop(0, NJ, phase_a, 0)
-    send_across(NJ - 1)
+        part = jnp.dot(ctx[...], wbuf[step % n_wo], preferred_element_type=F32)
+        return part
+
+    def refill(step):
+        if n_wo < 4 * NJ:
+            @pl.when(step + n_wo < 4 * NJ)
+            def _():
+                wo_copy(step + n_wo).start()
+        if fuse:
+            @pl.when(step >= 2 * NJ)
+            def _():
+                start_q(step - 2 * NJ + Q_FIRST)
+
+    def send_across(t):
+        part = (t % NJ, rows_of(t // NJ))
+        pair_a(t).wait_recv()
+        send_c[part] += recv_a[part]
+        across(t).start()
+
+    def half_sum(step, h):
+        @pl.when(h == 0)
+        def _():
+            wo_copy(step).wait()
+        return jnp.dot(ctx[rows_of(h), :], wbuf[step], preferred_element_type=F32)
+
+    context(1).wait_recv()
+
+    def phase_a(t, _):
+        h, j = t // NJ, t % NJ
+
+        @pl.when(t == NJ)
+        def _():
+            context(2).wait_recv()
+            context(3).wait_recv()
+        send_a[j, rows_of(h), :] = half_sum(2 * j, h)
+        pair_a(t).start()
+
+        @pl.when(t > 0)
+        def _():
+            send_across(t - 1)
+        send_c[j, rows_of(h), :] = half_sum(2 * j + 1, h)
+
+        @pl.when(h == 1)
+        def _():
+            refill(2 * j)
+            refill(2 * j + 1)
+        return 0
+
+    lax.fori_loop(0, 2 * NJ, phase_a, 0)
+    send_across(2 * NJ - 1)
 
     def phase_b(j, _):
         step = 2 * NJ + 2 * j
         send_b[j] = part_sum(step)
         pair_b(j).start()
+        refill(step)
         own[j] = part_sum(step + 1)
-        if fuse:
-            @pl.when(j >= NJ - 2)
-            def _():
-                start_q(2 * (j - NJ + 2))
-                start_q(2 * (j - NJ + 2) + 1)
-
-            @pl.when(j == NJ - 1)
-            def _():
-                start_q(4)
-                start_q(5)
+        refill(step + 1)
         return 0
 
     lax.fori_loop(0, NJ, phase_b, 0)
@@ -507,10 +544,11 @@
             for cp in q_copies(slot):
                 cp.wait()
 
-            @pl.when(slot + Q_AHEAD < 4 * NJ)
+            acc[...] += jnp.dot(hid[:, cols(chunk)], qbuf[slot % Q_SLOTS], preferred_element_type=F32)
+
+            @pl.when(slot + Q_SLOTS < 4 * NJ)
             def _():
-                start_q(slot + Q_AHEAD)
-            acc[...] += jnp.dot(hid[:, cols(chunk)], qbuf[slot], preferred_element_type=F32)
+                start_q(slot + Q_SLOTS)
 
     def from_partner(j):
         hidden(3, j, partner, partner).wait_recv()
@@ -518,7 +556,8 @@
 
     def phase_c(j, _):
         pair_b(j).wait_recv()
-        across(j).wait_recv()
+        across_here(j).wait_recv()
+        across_here(j + NJ).wait_recv()
         total = own[j] + recv_b[j] + recv_c[j]
         part = (resv[:, cols(j)].astype(F32) + total).astype(BF16)
         hid[:, cols(me * NJ + j)] = part
@@ -556,10 +595,14 @@
     if fuse:
         write_qkv(me, acc, q_outs, k_new, v_new)
 
+    for i in (1, 2, 3):
+        context(i).wait_send()
+
     def drain(j, _):
-        pair_a(j).wait_send()
+        for t in (j, j + NJ):
+            pair_a(t).wait_send()
+            across(t).wait_send()
         pair_b(j).wait_send()
-        across(j).wait_send()
         hidden(3, j, me, partner).wait_send()
         hidden(4, j, me, cross).wait_send()
         hidden(5, j, cross, partner).wait_send()
@@ -568,36 +611,35 @@
     lax.fori_loop(0, NJ, drain, 0)
 
 
-def out_product(layer, fuse, ds, res, w_out, qkv_weights):
+def out_product(layer, fuse, cs, res, w_out, qkv_weights):
     part = (NJ, ROWS, CH)
     shared = [
         VM((ROWS, QW), BF16),
         VM((ROWS, QW), BF16),
-        VM((WO_SLOTS, QW, CH), BF16),
+        VM((WO_SLOTS[layer], QW, CH), BF16),
         VM(part, F32), VM(part, F32), VM(part, F32), VM(part, F32), VM(part, F32), VM(part, F32), VM(part, F32),
-        pltpu.SemaphoreType.DMA((WO_SLOTS,)),
+        pltpu.SemaphoreType.DMA((WO_SLOTS[layer],)),
         pltpu.SemaphoreType.DMA,
-        pltpu.SemaphoreType.DMA((6, NJ)),
-        pltpu.SemaphoreType.DMA((6, NJ)),
+        pltpu.SemaphoreType.DMA((7, 2 * NJ)),
+        pltpu.SemaphoreType.DMA((7, 2 * NJ)),
     ]
-    n = D // CH
     flops = 2 * ROWS * QW * D
     if fuse:
         out_shape = [sds((MINE, QW))] * 4 + [sds((MINE, HD))] * 2 + [sds((ROWS, QW))]
         out_specs = [VSPEC] * 7
         extra = [
             VM((ROWS, D), BF16),
-            VM((n, CH, QKV), BF16),
+            VM((Q_SLOTS, CH, QKV), BF16),
             VM((ROWS, QKV), F32),
-            pltpu.SemaphoreType.DMA((3, n)),
+            pltpu.SemaphoreType.DMA((3, Q_SLOTS)),
         ]
-        args = (*ds, res, w_out, *qkv_weights)
+        args = (*cs, res, w_out, *qkv_weights)
         flops += 2 * ROWS * D * QKV
     else:
         out_shape = sds((ROWS, D))
         out_specs = VSPEC
         extra = []
-        args = (*ds, res, w_out)
+        args = (*cs, res, w_out)
     return pl.pallas_call(
         functools.partial(out_kernel, layer, fuse),
         out_shape=out_shape,
@@ -605,7 +647,7 @@
         out_specs=out_specs,
         scratch_shapes=extra + shared,
         compiler_params=pltpu.CompilerParams(
-            vmem_limit_bytes=53 * MIB if fuse else 32 * MIB, collective_id=layer, has_side_effects=True),
+            vmem_limit_bytes=53 * MIB if fuse else 44 * MIB, collective_id=layer, has_side_effects=True),
         cost_estimate=pl.CostEstimate(flops=flops, bytes_accessed=flops // ROWS, transcendentals=0),
         name=f"out_product_{layer}",
     )(*args)
@@ -629,13 +671,11 @@
                 k_out = copy_cache(layer, 0, K_CUT[layer], cache_len, k_new, k_cache, k_out)
                 priors = (k_out, v_out)
             *cs, k_out, v_out = attend(layer, cache_len, rs, k_new, v_new, k_cache, v_cache, priors)
-            ds = swap(cs)
-            v_out = copy_cache(layer, V_CUT[layer], MINE, cache_len, v_new, v_cache, v_out)
             if layer == 0:
-                *qs, k_new, v_new, res = out_product(0, True, ds, x, w_out, (w_query, w_key, w_value))
+                *qs, k_new, v_new, res = out_product(0, True, cs, x, w_out, (w_query, w_key, w_value))
                 rs = swap(qs)
             else:
-                out = out_product(1, False, ds, res, w_out, ())
+                out = out_product(1, False, cs, res, w_out, ())
         return out, k_out, v_out
 
     return jax.shard_map(

time: 107 us -> 101 us (0.944)
  starting transfers between devices: 5.62 us -> 1.88 us
  Pallas kernels: 99.5 us -> 97.6 us
    pallas_call x3 -> x1, Pallas kernels: 10.5 us -> 3.51 us  [copy_cache(): pl.pallas_call(functools.partial(copy_kernel, layer, first, last, len(arg...]
    ppermute x9 -> x3, starting transfers between devices: 5.62 us -> 1.88 us  [swap(): lax.ppermute(parts[i], 'model', [(m, m ^ i) for m in range(GROUPS)])]
    pallas_call x2, Pallas kernels: 48.6 us -> 51.2 us  [out_product(): pl.pallas_call(functools.partial(out_kernel, layer, fuse), out_shape=out_...]
    pallas_call x2, Pallas kernels: 22.9 us -> 25.3 us  [attend(): pl.pallas_call(functools.partial(attend_kernel, layer, len(args)), out_sh...]
  transfers between devices with their start and end apart: 9 -> 3, of which waited for: 2 -> 0; matrix products, arithmetic and copies ran while one was open for 0% -> 0% of each run, Pallas kernels for 10% -> 3%
where the time goes in v2:
time: 101 us
  Pallas kernels  97.6 us (97%)
  starting transfers between devices  1.88 us (2%)
    pallas_call x2, Pallas kernels, out_product(): pl.pallas_call(functools.partial(out_kernel, layer, fuse), out_shape=out_...  51.2 us
    pallas_call x2, Pallas kernels, attend(): pl.pallas_call(functools.partial(attend_kernel, layer, len(args)), out_sh...  25.3 us
    pallas_call x1, Pallas kernels, first_qkv(): pl.pallas_call(first_qkv_kernel, out_shape=[sds((MINE, QW))] * 4 + [sds((...  17.6 us
    pallas_call x1, Pallas kernels, copy_cache(): pl.pallas_call(functools.partial(copy_kernel, layer, first, last, len(arg...  3.51 us
  transfers between devices with their start and end apart: 3, of which 0 were waited for; matrix products, arithmetic and copies ran while one was open for 0% of the time, Pallas kernels for 3%

profile of v2, /device:TPU:0, one launch (start us, length us, event | category | flops | bytes accessed | tf_op | source)
XLA Modules:
  0.0 101.2 jit_solution(10919314277549301579)
XLA Ops:
  0.6 0.0 copy-start
  0.6 17.6 %first_qkv.1 = (bf16[16,2048]{1,0:T(8,128)(2,1)S(1)}, bf16[16,2048]{1,0:T(8,128)(2,1)S(1)}, bf16[16,2048]{1,0:T(8,128)(2,1)S(1)}, bf16[16,2048]{1,0:T(8,128)(2,1...) custom-call(bf16[64,8192]{1,0:T(8,128)(2,1)} %refs_4_.1, bf16[2,8192,2048]{2,1,0:T(8,128)(2,1)} %refs_6_.1, ...), custom_call_target="tpu_custom_call" | custom-call | flops 2415919104 | bytes 37748736 | tf_op jit(solution)/shard_map/first_qkv/pallas_call | solution.py:161
  18.2 0.0 copy-done
  18.2 13.5 %attend_0.1 = (bf16[16,2048]{1,0:T(8,128)(2,1)S(1)}, bf16[16,2048]{1,0:T(8,128)(2,1)S(1)}, bf16[16,2048]{1,0:T(8,128)(2,1)S(1)}, bf16[16,2048]{1,0:T(8,128)(2,1)...) custom-call(s32[64]{0:T(128)S(1)} %copy-done, ...), custom_call_target="tpu_custom_call" | custom-call | flops 5000000000 | bytes 8388608 | tf_op jit(solution)/shard_map/attend_0/pallas_call | solution.py:360
  31.7 26.0 %out_product_0.1 = (bf16[16,2048]{1,0:T(8,128)(2,1)S(1)}, bf16[16,2048]{1,0:T(8,128)(2,1)S(1)}, bf16[16,2048]{1,0:T(8,128)(2,1)S(1)}, bf16[16,2048]{1,0:T(8,128)...) custom-call(bf16[16,2048]{1,0:T(8,128)(2,1)S(1)} %get-tuple-element.34.refs_0_, ...), custom_call_target="tpu_custom_call" | custom-call | flops 4563402752 | bytes 71303168 | tf_op jit(solution)/shard_map/out_product_0/pallas_call | solution.py:643
  57.7 0.2 collective-permute-start
  57.9 0.7 collective-permute-start.1
  58.6 1.0 %collective-permute-start.2 = (bf16[16,2048]{1,0:T(8,128)(2,1)S(1)}, bf16[16,2048]{1,0:T(8,128)(2,1)S(1)}, u32[]{:S(2)}, u32[]{:S(2)}) collective-permute-start(bf16[16,2048]{1,0:T(8,128)(2,1)S(1)} %get-tuple-element.41), channel_id=1, source_target_pairs={{0,3},{1,2},{2,1},{3,0},{4,7},{5,6},{6,5},{7,4}} | collective-permute-start | bytes 196616 | tf_op jit(solution)/shard_map/ppermute | solution.py:659
  59.6 3.5 %copy_cache_1.1.refs_9_ = bf16[2,16,2048,128]{3,2,1,0:T(8,128)(2,1)} custom-call(s32[64]{0:T(128)S(1)} %copy-done, bf16[16,128]{1,0:T(8,128)(2,1)S(1)} %get-tuple-element.42.refs_1_.refs_5_, bf16[2,16,2048,128]{3,2,1,0:T(8,128)(2,1)} %refs_7_.5, bf16[2,16,2048,128]{3,2,1,0:T(8,128)(2,1)} %get-tuple-element.44.refs_3_), custom_call_target="tpu_custom_call", output_to_operand_aliasing={{}: (3, {})} | custom-call | flops 5000000000 | bytes 16777216 | tf_op jit(solution)/shard_map/copy_cache_1/pallas_call | solution.py:243
  63.1 0.0 collective-permute-done.refs_2_
  63.1 0.0 collective-permute-done.1.refs_3_
  63.2 0.0 collective-permute-done.2.refs_4_
  63.2 11.8 %attend_1.1 = (bf16[16,2048]{1,0:T(8,128)(2,1)S(1)}, bf16[16,2048]{1,0:T(8,128)(2,1)S(1)}, bf16[16,2048]{1,0:T(8,128)(2,1)S(1)}, bf16[16,2048]{1,0:T(8,128)(2,1)...) custom-call(s32[64]{0:T(128)S(1)} %copy-done, ...), custom_call_target="tpu_custom_call", output_to_operand_aliasing={{4}: (9, {}), {5}: (10, {})} | custom-call | flops 5000000000 | bytes 8388608 | tf_op jit(solution)/shard_map/attend_1/pallas_call | solution.py:360
  75.0 25.2 %out_product_1.1 = bf16[64,8192]{1,0:T(8,128)(2,1)S(1)} custom-call(bf16[16,2048]{1,0:T(8,128)(2,1)S(1)} %get-tuple-element.46.refs_0_, bf16[16,2048]{1,0:T(8,128)(2,1)S(1)} %get-tuple-element.47.refs_1_, bf16[16,2048]{1,0:T(8,128)(2,1)S(1)} %get-tuple-element.48.refs_2_, bf16[16,2048]{1,0:T(8,128)(2,1)S(1)} %get-tuple-element.49.refs_3_, ...), custom_call_target="tpu_custom_call" | custom-call | flops 2147483648 | bytes 33554432 | tf_op jit(solution)/shard_map/out_product_1/pallas_call | solution.py:643
  100.2 1.0 copy.18
Async XLA Ops:
  0.6 17.6 %copy-start = (s32[64]{0:T(128)S(1)}, s32[64]{0:T(128)}, u32[]{:S(2)}) copy-start(s32[64]{0:T(128)} %refs_0_.5) | copy-start | bytes 772
  57.7 5.4 %collective-permute-start = (bf16[16,2048]{1,0:T(8,128)(2,1)S(1)}, bf16[16,2048]{1,0:T(8,128)(2,1)S(1)}, u32[]{:S(2)}, u32[]{:S(2)}) collective-permute-start(bf16[16,2048]{1,0:T(8,128)(2,1)S(1)} %get-tuple-element.39), channel_id=1, source_target_pairs={{0,1},{1,0},{2,3},{3,2},{4,5},{5,4},{6,7},{7,6}} | collective-permute-start | bytes 196616 | tf_op jit(solution)/shard_map/ppermute | solution.py:659
  57.9 5.2 %collective-permute-start.1 = (bf16[16,2048]{1,0:T(8,128)(2,1)S(1)}, bf16[16,2048]{1,0:T(8,128)(2,1)S(1)}, u32[]{:S(2)}, u32[]{:S(2)}) collective-permute-start(bf16[16,2048]{1,0:T(8,128)(2,1)S(1)} %get-tuple-element.40), channel_id=1, source_target_pairs={{0,2},{1,3},{2,0},{3,1},{4,6},{5,7},{6,4},{7,5}} | collective-permute-start | bytes 196616 | tf_op jit(solution)/shard_map/ppermute | solution.py:659
  58.6 4.6 %collective-permute-start.2 = (bf16[16,2048]{1,0:T(8,128)(2,1)S(1)}, bf16[16,2048]{1,0:T(8,128)(2,1)S(1)}, u32[]{:S(2)}, u32[]{:S(2)}) collective-permute-start(bf16[16,2048]{1,0:T(8,128)(2,1)S(1)} %get-tuple-element.41), channel_id=1, source_target_pairs={{0,3},{1,2},{2,1},{3,0},{4,7},{5,6},{6,5},{7,4}} | collective-permute-start | bytes 196616 | tf_op jit(solution)/shard_map/ppermute | solution.py:659

commit v3 on v2

--- a/solution.py
+++ b/solution.py
@@ -10,7 +10,7 @@
 F32 = jnp.float32
 BF16 = jnp.bfloat16
 MIB = 1 << 20
-BIG = 50 * MIB
+BIG = 42 * MIB
 
 GROUPS = 4
 ROWS = 64
@@ -24,7 +24,7 @@
 NJ = QW // CH
 QKV = QW + 2 * HD
 WO_SLOTS = (8, 16)
-Q_SLOTS = 12
+Q_SLOTS = 8
 AHEAD = 4
 Q_FIRST = 4
 BLK = 256
@@ -45,15 +45,6 @@
         pltpu.make_async_copy(wk.at[layer, rows, :], buf.at[slot, :, pl.ds(QW, HD)], sems.at[1, slot]),
         pltpu.make_async_copy(wv.at[layer, rows, :], buf.at[slot, :, pl.ds(QW + HD, HD)], sems.at[2, slot]),
     )
-
-
-def write_qkv(me, acc, q_outs, k_new, v_new):
-    for i, q_out in enumerate(q_outs):
-        other = xor_id(me, i)
-        q_out[...] = acc[pl.ds(pl.multiple_of(other * MINE, MINE), MINE), 0:QW].astype(BF16)
-    mine = pl.ds(pl.multiple_of(me * MINE, MINE), MINE)
-    k_new[...] = acc[mine, QW:QW + HD].astype(BF16)
-    v_new[...] = acc[mine, QW + HD:QKV].astype(BF16)
 
 
 def xor_id(me, i):
@@ -66,8 +57,13 @@
     return other
 
 
-def first_qkv_kernel(x, wq, wk, wv, r0, r1, r2, r3, k_new, v_new,
-                     xbuf, wbuf, kvbuf, acc, qbuf, rbuf, x_sem, w_sems, kv_sems, ssems, rsems):
+def read_keys(layer, k_cache, keys, sems, act):
+    for b in range(MINE):
+        act(pltpu.make_async_copy(k_cache.at[layer, b], keys.at[b], sems.at[b]))
+
+
+def first_qkv_kernel(x, wq, wk, wv, k_cache, r0, r1, r2, r3, k_new, v_new, keys,
+                     xbuf, wbuf, kvbuf, acc, qbuf, rbuf, x_sem, w_sems, kv_sems, k_sems, ssems, rsems):
     me = lax.axis_index("model")
     depth = D // NJ
 
@@ -110,6 +106,10 @@
             @pl.when(n * NJ + k + AHEAD < NJ * NJ)
             def _():
                 w_copy(n * NJ + k + AHEAD).start()
+
+            @pl.when(n * NJ + k == NJ * NJ - 1)
+            def _():
+                read_keys(0, k_cache, keys, k_sems, lambda cp: cp.start())
             part = xbuf[:, pl.ds(pl.multiple_of(k * depth, depth), depth)]
             acc[...] += jnp.dot(part, wbuf[n * NJ + k], preferred_element_type=F32)
             return 0
@@ -148,6 +148,7 @@
         for n in range(NJ):
             send(i, n).wait_recv()
         r[...] = rbuf[i - 1]
+    read_keys(0, k_cache, keys, k_sems, lambda cp: cp.wait())
 
     def drain(n, _):
         for i in range(1, GROUPS):
@@ -157,12 +158,12 @@
     lax.fori_loop(0, NJ, drain, 0)
 
 
-def first_qkv(x, wq, wk, wv):
+def first_qkv(x, wq, wk, wv, k_cache):
     return pl.pallas_call(
         first_qkv_kernel,
-        out_shape=[sds((MINE, QW))] * 4 + [sds((MINE, HD))] * 2,
-        in_specs=[ASPEC] * 4,
-        out_specs=[VSPEC] * 6,
+        out_shape=[sds((MINE, QW))] * 4 + [sds((MINE, HD))] * 2 + [VM((MINE, SEQ, HD), BF16)],
+        in_specs=[ASPEC] * 5,
+        out_specs=[VSPEC] * 7,
         scratch_shapes=[
             VM((ROWS, D), BF16),
             VM((NJ * NJ, D // NJ, CH), BF16),
@@ -173,97 +174,34 @@
             pltpu.SemaphoreType.DMA,
             pltpu.SemaphoreType.DMA((NJ * NJ,)),
             pltpu.SemaphoreType.DMA((2,)),
+            pltpu.SemaphoreType.DMA((MINE,)),
             pltpu.SemaphoreType.DMA((GROUPS - 1, NJ)),
             pltpu.SemaphoreType.DMA((GROUPS - 1, NJ)),
         ],
-        compiler_params=pltpu.CompilerParams(vmem_limit_bytes=53 * MIB, collective_id=2, has_side_effects=True),
+        compiler_params=pltpu.CompilerParams(vmem_limit_bytes=BIG, collective_id=2, has_side_effects=True),
         cost_estimate=pl.CostEstimate(flops=2 * ROWS * D * QKV, bytes_accessed=2 * D * QKV, transcendentals=0),
         name="first_qkv",
-    )(x, wq, wk, wv)
-
-
-K_CUT = (0, 6)
-V_CUT = (16, 16)
-READ_AHEAD = 2
-
-
-def put_row(buf, b, length, row):
-    base = pl.multiple_of((length // 16) * 16, 16)
-    here = lax.broadcasted_iota(jnp.int32, (16, HD), 0) == length - base
-    buf[b, pl.ds(base, 16), :] = jnp.where(here, row, buf[b, pl.ds(base, 16), :])
-
-
-class Share:
-    def __init__(self, layer, first, last, lens, new, src, dst, buf, in_sems, out_sems):
-        self.layer, self.first, self.count = layer, first, last - first
-        self.lens, self.new, self.src, self.dst, self.buf = lens, new, src, dst, buf
-        self.in_sems, self.out_sems = in_sems, out_sems
-
-    def take(self, n):
-        return pltpu.make_async_copy(self.src.at[self.layer, self.first + n], self.buf.at[n], self.in_sems.at[n])
-
-    def give(self, n):
-        return pltpu.make_async_copy(self.buf.at[n], self.dst.at[self.layer, self.first + n], self.out_sems.at[n])
-
-    def start(self):
-        for n in range(self.count):
-            self.take(n).start()
-
-    def forward(self, n):
-        me = lax.axis_index("model")
-        self.take(n).wait()
-        b = self.first + n
-        put_row(self.buf, n, self.lens[me * MINE + b], self.new[pl.ds(b, 1), :])
-        if n:
-            self.give(n - 1).start()
-        if n == self.count - 1:
-            self.give(n).start()
-
-    def finish(self):
-        for n in range(self.count):
-            self.give(n).wait()
-
-    @staticmethod
-    def scratch(first, last):
-        return [VM((last - first, SEQ, HD), BF16), pltpu.SemaphoreType.DMA((last - first,)),
-                pltpu.SemaphoreType.DMA((last - first,))]
-
-
-def copy_kernel(layer, first, last, n_in, *refs):
-    lens, new, src = refs[:3]
-    share = Share(layer, first, last, lens, new, src, *refs[n_in:])
-    share.start()
-    for n in range(share.count):
-        share.forward(n)
-    share.finish()
-
-
-def copy_cache(layer, first, last, lens, new, src, prior):
-    args = [lens, new, src] + ([prior] if prior is not None else [])
-    return pl.pallas_call(
-        functools.partial(copy_kernel, layer, first, last, len(args)),
-        out_shape=sds(src.shape),
-        in_specs=[SSPEC, VSPEC, ASPEC] + ([ASPEC] if prior is not None else []),
-        out_specs=ASPEC,
-        input_output_aliases={3: 0} if prior is not None else {},
-        scratch_shapes=Share.scratch(first, last),
-        compiler_params=pltpu.CompilerParams(vmem_limit_bytes=BIG),
-        cost_estimate=pl.CostEstimate(flops=5_000_000_000, bytes_accessed=4 * MINE * SEQ * HD, transcendentals=0),
-        name=f"copy_cache_{layer}",
-    )(*args)
+    )(x, wq, wk, wv, k_cache)
 
 
 GRP = 8
 TIERS = (512, 1024, 2048)
 
 
+def aligned(length):
+    return pl.ds(pl.multiple_of((length // 16) * 16, 16), 16)
+
+
+def with_row(block, length, row):
+    return jnp.where(lax.broadcasted_iota(jnp.int32, (16, HD), 0) == length % 16, row, block)
+
+
 def attend_kernel(layer, n_in, *refs):
-    lens, r0, r1, r2, r3, k_new, v_new, k_cache, v_cache = refs[:9]
-    c0, c1, c2, c3, k_out, v_out, kbuf, vbuf, qbuf, cbuf, new_kv, ksems, vsems, ko_sems, vo_sems = refs[n_in:]
+    lens, r0, r1, r2, r3, k_new, v_new, keys, v_cache = refs[:9]
+    c0, c1, c2, c3, k_out, v_out, vbuf, qbuf, cbuf, new_kv, patch, v_sems, ko_sems, vo_sems, p_sems = refs[n_in:]
     me = lax.axis_index("model")
     n_heads = GROUPS * LH
     scale = HD ** -0.5
-    caches = ((k_cache, kbuf, ksems, k_out, ko_sems, K_CUT[layer], MINE), (v_cache, vbuf, vsems, v_out, vo_sems, 0, V_CUT[layer]))
 
     def length(b):
         return lens[me * MINE + b]
@@ -271,39 +209,26 @@
     def tier_of(b, n):
         return jnp.logical_and(length(b) < TIERS[n], length(b) >= (TIERS[n - 1] if n else BLK))
 
-    def reads(b, act):
-        for cache, buf, sems, _, _, first, last in caches:
-            def part(start, size, cache=cache, buf=buf, sems=sems):
-                cut = pl.ds(start, size)
-                return pltpu.make_async_copy(cache.at[layer, b, cut, :], buf.at[b, cut, :], sems.at[b, min(start, 1)])
-
-            @pl.when(jnp.logical_and(b >= first, b < last))
-            def _(part=part):
-                act(part(0, SEQ))
-
-            @pl.when(jnp.logical_or(b < first, b >= last))
-            def _(part=part):
-                act(part(0, BLK))
-                for n, size in enumerate(TIERS):
-                    @pl.when(tier_of(b, n))
-                    def _(size=size):
-                        act(part(BLK, size - BLK))
-
-    def writes(b, act):
-        for _, buf, _, out, sems, first, last in caches:
-            @pl.when(jnp.logical_and(b >= first, b < last))
-            def _(buf=buf, out=out, sems=sems):
-                act(pltpu.make_async_copy(buf.at[b], out.at[layer, b], sems.at[b]))
-
-    def each(g, do):
-        for i in range(GRP):
-            do(g * GRP + i)
-
-    def start_group(g, _):
-        each(g, lambda b: reads(b, lambda cp: cp.start()))
-        return 0
-
-    lax.fori_loop(0, READ_AHEAD, start_group, 0)
+    def v_read(b):
+        return pltpu.make_async_copy(v_cache.at[layer, b], vbuf.at[b], v_sems.at[b])
+
+    def v_write(b):
+        return pltpu.make_async_copy(vbuf.at[b], v_out.at[layer, b], vo_sems.at[b])
+
+    def k_write(b):
+        return pltpu.make_async_copy(keys.at[b], k_out.at[layer, b], ko_sems.at[b])
+
+    def k_patch(b):
+        return pltpu.make_async_copy(patch.at[b], k_out.at[layer, b, aligned(length(b)), :], p_sems.at[b])
+
+    def each(do):
+        def step(b, _):
+            do(b)
+            return 0
+        lax.fori_loop(0, MINE, step, 0)
+
+    each(lambda b: v_read(b).start())
+    each(lambda b: k_write(b).start())
     for i, r in enumerate((r0, r1, r2, r3)):
         qbuf[:, i * LH:(i + 1) * LH, :] = r[...].reshape(MINE, LH, HD)
     for b in range(MINE):
@@ -313,19 +238,16 @@
     def context(seqs, size):
         scores = []
         for b in seqs:
-            s = lax.dot_general(qbuf[b], kbuf[b, 0:size, :], (((1,), (1,)), ((), ())), preferred_element_type=F32)
+            s = lax.dot_general(qbuf[b], keys[b, 0:size, :], (((1,), (1,)), ((), ())), preferred_element_type=F32)
+            s_new = jnp.sum(qbuf[b].astype(F32) * new_kv[0, b], axis=1, keepdims=True)
             pos = lax.broadcasted_iota(jnp.int32, (n_heads, size), 1)
+            s = jnp.where(pos == length(b), s_new, s)
             scores.append(jnp.where(pos <= length(b), s * scale, -jnp.inf))
         expos = [jnp.exp(s - jnp.max(s, axis=1, keepdims=True)) for s in scores]
         probs = [(e * (1.0 / jnp.sum(e, axis=1, keepdims=True))).astype(BF16) for e in expos]
         for b, p in zip(seqs, probs):
             cbuf[b] = jnp.dot(p, vbuf[b, 0:size, :], preferred_element_type=F32).astype(BF16)
 
-    def ready(b):
-        reads(b, lambda cp: cp.wait())
-        put_row(kbuf, b, length(b), new_kv[0, b].astype(BF16))
-        put_row(vbuf, b, length(b), new_kv[1, b].astype(BF16))
-
     def long_one(b, _):
         for n, size in enumerate(TIERS):
             @pl.when(tier_of(b, n))
@@ -334,48 +256,48 @@
         return 0
 
     def group(g, _):
-        each(g, ready)
-
-        @pl.when(g + READ_AHEAD < MINE // GRP)
-        def _():
-            start_group(g + READ_AHEAD, 0)
-        context([g * GRP + i for i in range(GRP)], BLK)
-        each(g, lambda b: writes(b, lambda cp: cp.start()))
+        seqs = [g * GRP + i for i in range(GRP)]
+        for b in seqs:
+            rows = aligned(length(b))
+            patch[b] = with_row(keys[b, rows, :], length(b), new_kv[0, b].astype(BF16))
+            v_read(b).wait()
+            vbuf[b, rows, :] = with_row(vbuf[b, rows, :], length(b), new_kv[1, b].astype(BF16))
+        context(seqs, BLK)
+        for b in seqs:
+            v_write(b).start()
+            k_write(b).wait()
+            k_patch(b).start()
         lax.fori_loop(g * GRP, (g + 1) * GRP, long_one, 0)
         return 0
 
     lax.fori_loop(0, MINE // GRP, group, 0)
     for i, c in enumerate((c0, c1, c2, c3)):
         c[...] = cbuf[:, i * LH:(i + 1) * LH, :].reshape(MINE, QW)
-
-    def finish(b, _):
-        writes(b, lambda cp: cp.wait())
-        return 0
-
-    lax.fori_loop(0, MINE, finish, 0)
-
-
-def attend(layer, lens, rs, k_new, v_new, k_cache, v_cache, priors):
-    args = [lens, *rs, k_new, v_new, k_cache, v_cache, *priors]
+    each(lambda b: v_write(b).wait())
+    each(lambda b: k_patch(b).wait())
+
+
+def attend(layer, lens, rs, k_new, v_new, keys, v_cache, priors):
+    args = [lens, *rs, k_new, v_new, keys, v_cache, *priors]
     return pl.pallas_call(
         functools.partial(attend_kernel, layer, len(args)),
-        out_shape=[sds((MINE, QW))] * 4 + [sds(k_cache.shape)] * 2,
-        in_specs=[SSPEC] + [VSPEC] * 6 + [ASPEC] * (len(args) - 7),
+        out_shape=[sds((MINE, QW))] * 4 + [sds(v_cache.shape)] * 2,
+        in_specs=[SSPEC] + [VSPEC] * 7 + [ASPEC] * (len(args) - 8),
         out_specs=[VSPEC] * 4 + [ASPEC] * 2,
         input_output_aliases={9: 4, 10: 5} if priors else {},
         scratch_shapes=[
             VM((MINE, SEQ, HD), BF16),
-            VM((MINE, SEQ, HD), BF16),
             VM((MINE, GROUPS * LH, HD), BF16),
             VM((MINE, GROUPS * LH, HD), BF16),
             VM((2, MINE, 1, HD), F32),
-            pltpu.SemaphoreType.DMA((MINE, 2)),
-            pltpu.SemaphoreType.DMA((MINE, 2)),
+            VM((MINE, 16, HD), BF16),
+            pltpu.SemaphoreType.DMA((MINE,)),
+            pltpu.SemaphoreType.DMA((MINE,)),
             pltpu.SemaphoreType.DMA((MINE,)),
             pltpu.SemaphoreType.DMA((MINE,)),
         ],
         compiler_params=pltpu.CompilerParams(vmem_limit_bytes=BIG),
-        cost_estimate=pl.CostEstimate(flops=5_000_000_000, bytes_accessed=8 * MIB, transcendentals=0),
+        cost_estimate=pl.CostEstimate(flops=5_000_000_000, bytes_accessed=24 * MIB, transcendentals=0),
         name=f"attend_{layer}",
     )(*args)
 
@@ -383,10 +305,10 @@
 def out_kernel(layer, fuse, *refs):
     c_refs, (res, wo), refs = refs[:4], refs[4:6], refs[6:]
     if fuse:
-        (wq, wk, wv), outs, refs = refs[:3], refs[3:10], refs[10:]
-        q_outs, (k_new, v_new, res_out) = outs[:4], outs[4:]
-        hid, qbuf, acc, q_sems = refs[:4]
-        refs = refs[4:]
+        (wq, wk, wv, k_cache), outs, refs = refs[:4], refs[4:12], refs[12:]
+        r_outs, (k_new, v_new, res_out, keys) = outs[:4], outs[4:]
+        hid, qbuf, acc, q_all, rbuf, q_sems, k_sems = refs[:7]
+        refs = refs[7:]
     else:
         hid, refs = refs[0], refs[1:]
     ctx, resv, wbuf, send_a, recv_a, send_c, recv_c, send_b, recv_b, own, w_sems, res_sem, ssems, rsems = refs
@@ -484,9 +406,11 @@
             def _():
                 wo_copy(step + n_wo).start()
         if fuse:
-            @pl.when(step >= 2 * NJ)
+            slot = step - 2 * NJ + Q_FIRST
+
+            @pl.when(jnp.logical_and(step >= 2 * NJ, slot < Q_SLOTS))
             def _():
-                start_q(step - 2 * NJ + Q_FIRST)
+                start_q(slot)
 
     def send_across(t):
         part = (t % NJ, rows_of(t // NJ))
@@ -590,11 +514,29 @@
         return 0
 
     lax.fori_loop(0, NJ, phase_d, 0)
+    if fuse:
+        read_keys(layer + 1, k_cache, keys, k_sems, lambda cp: cp.start())
     forwarded(NJ - 1)
 
     if fuse:
-        write_qkv(me, acc, q_outs, k_new, v_new)
-
+        def query(i):
+            dev = xor_id(me, i)
+            rows = pl.ds(pl.multiple_of(dev * MINE, MINE), MINE)
+            return send(6, GROUPS + i, q_all.at[rows, :], rbuf.at[i - 1], dev)
+
+        q_all[...] = acc[:, 0:QW].astype(BF16)
+        for i in (3, 2, 1):
+            query(i).start()
+        mine = pl.ds(pl.multiple_of(me * MINE, MINE), MINE)
+        k_new[...] = acc[mine, QW:QW + HD].astype(BF16)
+        v_new[...] = acc[mine, QW + HD:QKV].astype(BF16)
+        r_outs[0][...] = q_all[mine, :]
+        for i in (1, 2, 3):
+            query(i).wait_recv()
+            r_outs[i][...] = rbuf[i - 1]
+        read_keys(layer + 1, k_cache, keys, k_sems, lambda cp: cp.wait())
+        for i in (1, 2, 3):
+            query(i).wait_send()
     for i in (1, 2, 3):
         context(i).wait_send()
 
@@ -625,13 +567,16 @@
     ]
     flops = 2 * ROWS * QW * D
     if fuse:
-        out_shape = [sds((MINE, QW))] * 4 + [sds((MINE, HD))] * 2 + [sds((ROWS, QW))]
-        out_specs = [VSPEC] * 7
+        out_shape = [sds((MINE, QW))] * 4 + [sds((MINE, HD))] * 2 + [sds((ROWS, QW)), VM((MINE, SEQ, HD), BF16)]
+        out_specs = [VSPEC] * 8
         extra = [
             VM((ROWS, D), BF16),
             VM((Q_SLOTS, CH, QKV), BF16),
             VM((ROWS, QKV), F32),
+            VM((ROWS, QW), BF16),
+            VM((GROUPS - 1, MINE, QW), BF16),
             pltpu.SemaphoreType.DMA((3, Q_SLOTS)),
+            pltpu.SemaphoreType.DMA((MINE,)),
         ]
         args = (*cs, res, w_out, *qkv_weights)
         flops += 2 * ROWS * D * QKV
@@ -647,35 +592,22 @@
         out_specs=out_specs,
         scratch_shapes=extra + shared,
         compiler_params=pltpu.CompilerParams(
-            vmem_limit_bytes=53 * MIB if fuse else 44 * MIB, collective_id=layer, has_side_effects=True),
+            vmem_limit_bytes=44 * MIB, collective_id=layer, has_side_effects=True),
         cost_estimate=pl.CostEstimate(flops=flops, bytes_accessed=flops // ROWS, transcendentals=0),
         name=f"out_product_{layer}",
     )(*args)
 
 
-def swap(parts):
-    out = [parts[0]]
-    for i in range(1, GROUPS):
-        out.append(lax.ppermute(parts[i], "model", [(m, m ^ i) for m in range(GROUPS)]))
-    return out
-
-
 def solution(mesh):
     cache_spec = P(None, ("replica", "model"), None, None)
 
     def device_step(x, cache_len, w_query, w_key, w_value, w_out, k_cache, v_cache):
-        *rs, k_new, v_new = first_qkv(x, w_query, w_key, w_value)
-        priors = ()
-        for layer in range(2):
-            if layer:
-                k_out = copy_cache(layer, 0, K_CUT[layer], cache_len, k_new, k_cache, k_out)
-                priors = (k_out, v_out)
-            *cs, k_out, v_out = attend(layer, cache_len, rs, k_new, v_new, k_cache, v_cache, priors)
-            if layer == 0:
-                *qs, k_new, v_new, res = out_product(0, True, cs, x, w_out, (w_query, w_key, w_value))
-                rs = swap(qs)
-            else:
-                out = out_product(1, False, cs, res, w_out, ())
+        x = pltpu.with_memory_space_constraint(x, pltpu.HBM)
+        *rs, k_new, v_new, keys = first_qkv(x, w_query, w_key, w_value, k_cache)
+        *cs, k_out, v_out = attend(0, cache_len, rs, k_new, v_new, keys, v_cache, ())
+        *rs, k_new, v_new, res, keys = out_product(0, True, cs, x, w_out, (w_query, w_key, w_value, k_cache))
+        *cs, k_out, v_out = attend(1, cache_len, rs, k_new, v_new, keys, v_cache, (k_out, v_out))
+        out = out_product(1, False, cs, res, w_out, ())
         return out, k_out, v_out
 
     return jax.shard_map(

time: 101 us -> 97.8 us (0.968)
  starting transfers between devices: 1.88 us -> 0 us
  Pallas kernels: 97.6 us -> 96.5 us
    pallas_call x2, Pallas kernels: 51.2 us -> 58.1 us  [out_product(): pl.pallas_call(functools.partial(out_kernel, layer, fuse), out_shape=out_...]
    pallas_call x2, Pallas kernels: 25.3 us -> 20.6 us  [attend(): pl.pallas_call(functools.partial(attend_kernel, layer, len(args)), out_sh...]
    pallas_call x1 -> x0, Pallas kernels: 3.51 us -> none  [copy_cache(): pl.pallas_call(functools.partial(copy_kernel, layer, first, last, len(arg...]
    ppermute x3 -> x0, starting transfers between devices: 1.88 us -> none  [swap(): lax.ppermute(parts[i], 'model', [(m, m ^ i) for m in range(GROUPS)])]
  transfers between devices with their start and end apart: 3 -> 0, of which waited for: 0 -> 0; matrix products, arithmetic and copies ran while one was open for 0% -> 0% of each run, Pallas kernels for 3% -> 0%
where the time goes in v3:
time: 97.8 us; the launch traced here: 98.1 us
  Pallas kernels  96.5 us (99%)
  local copies, waits for them, and re-layouts  0.98 us (1%)
    pallas_call x2, Pallas kernels, out_product(): pl.pallas_call(functools.partial(out_kernel, layer, fuse), out_shape=out_...  58.1 us
    pallas_call x2, Pallas kernels, attend(): pl.pallas_call(functools.partial(attend_kernel, layer, len(args)), out_sh...  20.6 us
    pallas_call x1, Pallas kernels, first_qkv(): pl.pallas_call(first_qkv_kernel, out_shape=[sds((MINE, QW))] * 4 + [sds((...  17.7 us

profile of v3, /device:TPU:0, one launch (start us, length us, event | category | flops | bytes accessed | tf_op | source)
XLA Modules:
  0.0 98.1 jit_solution(11844686722861879857)
XLA Ops:
  0.6 0.0 copy-start
  0.6 17.7 %first_qkv.1 = (bf16[16,2048]{1,0:T(8,128)(2,1)S(1)}, bf16[16,2048]{1,0:T(8,128)(2,1)S(1)}, bf16[16,2048]{1,0:T(8,128)(2,1)S(1)}, bf16[16,2048]{1,0:T(8,128)(2,1...) custom-call(bf16[64,8192]{1,0:T(8,128)(2,1)} %refs_4_.1, ...), custom_call_target="tpu_custom_call" | custom-call | flops 2415919104 | bytes 37748736 | tf_op jit(solution)/shard_map/first_qkv/pallas_call | solution.py:162
  18.4 0.0 copy-done
  18.4 10.3 %attend_0.1 = (bf16[16,2048]{1,0:T(8,128)(2,1)S(1)}, bf16[16,2048]{1,0:T(8,128)(2,1)S(1)}, bf16[16,2048]{1,0:T(8,128)(2,1)S(1)}, bf16[16,2048]{1,0:T(8,128)(2,1)...) custom-call(s32[64]{0:T(128)S(1)} %copy-done, ...), custom_call_target="tpu_custom_call" | custom-call | flops 5000000000 | bytes 25165824 | tf_op jit(solution)/shard_map/attend_0/pallas_call | solution.py:282
  28.7 31.9 %out_product_0.1 = (bf16[16,2048]{1,0:T(8,128)(2,1)S(1)}, bf16[16,2048]{1,0:T(8,128)(2,1)S(1)}, bf16[16,2048]{1,0:T(8,128)(2,1)S(1)}, bf16[16,2048]{1,0:T(8,128)...) custom-call(bf16[16,2048]{1,0:T(8,128)(2,1)S(1)} %get-tuple-element., ...), custom_call_target="tpu_custom_call" | custom-call | flops 4563402752 | bytes 71303168 | tf_op jit(solution)/shard_map/out_product_0/pallas_call | solution.py:588
  60.5 10.3 %attend_1.1 = (bf16[16,2048]{1,0:T(8,128)(2,1)S(1)}, bf16[16,2048]{1,0:T(8,128)(2,1)S(1)}, bf16[16,2048]{1,0:T(8,128)(2,1)S(1)}, bf16[16,2048]{1,0:T(8,128)(2,1)...) custom-call(s32[64]{0:T(128)S(1)} %copy-done, ...), custom_call_target="tpu_custom_call", output_to_operand_aliasing={{4}: (9, {}), {5}: (10, {})} | custom-call | flops 5000000000 | bytes 25165824 | tf_op jit(solution)/shard_map/attend_1/pallas_call | solution.py:282
  70.9 26.3 %out_product_1.1 = bf16[64,8192]{1,0:T(8,128)(2,1)S(1)} custom-call(bf16[16,2048]{1,0:T(8,128)(2,1)S(1)} %get-tuple-element.50.refs_0_, bf16[16,2048]{1,0:T(8,128)(2,1)S(1)} %get-tuple-element.51.refs_1_, bf16[16,2048]{1,0:T(8,128)(2,1)S(1)} %get-tuple-element.52.refs_2_, bf16[16,2048]{1,0:T(8,128)(2,1)S(1)} %get-tuple-element.53.refs_3_, ...), custom_call_target="tpu_custom_call" | custom-call | flops 2147483648 | bytes 33554432 | tf_op jit(solution)/shard_map/out_product_1/pallas_call | solution.py:588
  97.2 1.0 copy.16
Async XLA Ops:
  0.6 17.7 %copy-start = (s32[64]{0:T(128)S(1)}, s32[64]{0:T(128)}, u32[]{:S(2)}) copy-start(s32[64]{0:T(128)} %refs_0_.3) | copy-start | bytes 772

commit v4 on v3

--- a/solution.py
+++ b/solution.py
@@ -24,9 +24,12 @@
 NJ = QW // CH
 QKV = QW + 2 * HD
 WO_SLOTS = (8, 16)
-Q_SLOTS = 8
+Q_SLOTS = 6
 AHEAD = 4
 Q_FIRST = 4
+KEYS_AT = 14
+V_HELD = (0, 8)
+CACHES_AT = 2
 BLK = 256
 VM = pltpu.VMEM
 VSPEC = pl.BlockSpec(memory_space=pltpu.VMEM)
@@ -57,13 +60,13 @@
     return other
 
 
-def read_keys(layer, k_cache, keys, sems, act):
-    for b in range(MINE):
-        act(pltpu.make_async_copy(k_cache.at[layer, b], keys.at[b], sems.at[b]))
+def read_cache(count, cache, held, sems, act):
+    for b in range(count):
+        act(pltpu.make_async_copy(cache.at[b], held.at[b], sems.at[b]))
 
 
 def first_qkv_kernel(x, wq, wk, wv, k_cache, r0, r1, r2, r3, k_new, v_new, keys,
-                     xbuf, wbuf, kvbuf, acc, qbuf, rbuf, x_sem, w_sems, kv_sems, k_sems, ssems, rsems):
+                     xbuf, wbuf, kvbuf, acc, qbuf, rbuf, kvrows, kvback, x_sem, w_sems, kv_sems, k_sems, ssems, rsems):
     me = lax.axis_index("model")
     depth = D // NJ
 
@@ -84,7 +87,20 @@
 
     x_copy = pltpu.make_async_copy(x, xbuf, x_sem)
     x_copy.start()
-    kv_copies = [pltpu.make_async_copy(w.at[0], kvbuf.at[:, pl.ds(i * HD, HD)], kv_sems.at[i]) for i, w in enumerate((wk, wv))]
+    core = lax.rem(me, 2)
+
+    def kv_weight(act):
+        for i, w in enumerate((wk, wv)):
+            @pl.when(core == i)
+            def _(w=w):
+                act(pltpu.make_async_copy(w.at[0], kvbuf, kv_sems.at[0]))
+
+    def kv_send():
+        rows = pl.ds(pl.multiple_of((1 - core) * MINE, MINE), MINE)
+        return pltpu.make_async_remote_copy(
+            src_ref=kvrows.at[rows, :], dst_ref=kvback, send_sem=kv_sems.at[1], recv_sem=kv_sems.at[2],
+            device_id={"model": xor_id(me, 1)}, device_id_type=pl.DeviceIdType.MESH)
+
 
     def start(step, _):
         w_copy(step).start()
@@ -107,9 +123,9 @@
             def _():
                 w_copy(n * NJ + k + AHEAD).start()
 
-            @pl.when(n * NJ + k == NJ * NJ - 1)
+            @pl.when(n * NJ + k == KEYS_AT)
             def _():
-                read_keys(0, k_cache, keys, k_sems, lambda cp: cp.start())
+                read_cache(MINE, k_cache.at[0], keys, k_sems, lambda cp: cp.start())
             part = xbuf[:, pl.ds(pl.multiple_of(k * depth, depth), depth)]
             acc[...] += jnp.dot(part, wbuf[n * NJ + k], preferred_element_type=F32)
             return 0
@@ -128,27 +144,30 @@
     def later(n, _):
         @pl.when(n == NJ - 1)
         def _():
-            for cp in kv_copies:
-                cp.start()
+            kv_weight(lambda cp: cp.start())
         group(n)
         leave(n)
         return 0
 
     lax.fori_loop(1, NJ, later, 0)
     mine = pl.ds(pl.multiple_of(me * MINE, MINE), MINE)
-    for cp in kv_copies:
-        cp.wait()
-    kv = jnp.zeros((MINE, 2 * HD), F32)
+    kv_weight(lambda cp: cp.wait())
+    chip_rows = pl.ds(pl.multiple_of(lax.div(me, 2) * 2 * MINE, 2 * MINE), 2 * MINE)
+    kv = jnp.zeros((2 * MINE, HD), F32)
     for k in range(NJ):
-        kv += jnp.dot(xbuf[mine, k * depth:(k + 1) * depth], kvbuf[k * depth:(k + 1) * depth, :], preferred_element_type=F32)
-    k_new[...] = kv[:, :HD].astype(BF16)
-    v_new[...] = kv[:, HD:].astype(BF16)
+        kv += jnp.dot(xbuf[chip_rows, k * depth:(k + 1) * depth], kvbuf[k * depth:(k + 1) * depth, :], preferred_element_type=F32)
+    kvrows[...] = kv.astype(BF16)
+    kv_send().start()
     r0[...] = qbuf[mine, :]
     for i, r in ((1, r1), (2, r2), (3, r3)):
         for n in range(NJ):
             send(i, n).wait_recv()
         r[...] = rbuf[i - 1]
-    read_keys(0, k_cache, keys, k_sems, lambda cp: cp.wait())
+    kv_send().wait()
+    here = kvrows[pl.ds(pl.multiple_of(core * MINE, MINE), MINE), :]
+    k_new[...] = jnp.where(core == 0, here, kvback[...])
+    v_new[...] = jnp.where(core == 0, kvback[...], here)
+    read_cache(MINE, k_cache.at[0], keys, k_sems, lambda cp: cp.wait())
 
     def drain(n, _):
         for i in range(1, GROUPS):
@@ -167,13 +186,15 @@
         scratch_shapes=[
             VM((ROWS, D), BF16),
             VM((NJ * NJ, D // NJ, CH), BF16),
-            VM((D, 2 * HD), BF16),
+            VM((D, HD), BF16),
             VM((ROWS, CH), F32),
             VM((ROWS, QW), BF16),
             VM((GROUPS - 1, MINE, QW), BF16),
+            VM((2 * MINE, HD), BF16),
+            VM((MINE, HD), BF16),
             pltpu.SemaphoreType.DMA,
             pltpu.SemaphoreType.DMA((NJ * NJ,)),
-            pltpu.SemaphoreType.DMA((2,)),
+            pltpu.SemaphoreType.DMA((3,)),
             pltpu.SemaphoreType.DMA((MINE,)),
             pltpu.SemaphoreType.DMA((GROUPS - 1, NJ)),
             pltpu.SemaphoreType.DMA((GROUPS - 1, NJ)),
@@ -197,12 +218,19 @@
 
 
 def attend_kernel(layer, n_in, *refs):
-    lens, r0, r1, r2, r3, k_new, v_new, keys, v_cache = refs[:9]
-    c0, c1, c2, c3, k_out, v_out, vbuf, qbuf, cbuf, new_kv, patch, v_sems, ko_sems, vo_sems, p_sems = refs[n_in:]
+    lens, r0, r1, r2, r3, k_new, v_new = refs[:7]
+    c0, c1, c2, c3, k_out, v_out, qbuf, cbuf, new_kv, patch, out_sems, patch_sems = refs[n_in:n_in + 12]
+    keys = refs[7].at[pl.ds(0, MINE)]
+    v_cache = refs[8]
+    vbuf, v_sems = refs[n_in + 12:]
+    held = V_HELD[layer]
     me = lax.axis_index("model")
     n_heads = GROUPS * LH
     scale = HD ** -0.5
 
+    def value(b, held_group):
+        return refs[7].at[MINE + b] if held_group else vbuf.at[b - held]
+
     def length(b):
         return lens[me * MINE + b]
 
@@ -210,93 +238,117 @@
         return jnp.logical_and(length(b) < TIERS[n], length(b) >= (TIERS[n - 1] if n else BLK))
 
     def v_read(b):
-        return pltpu.make_async_copy(v_cache.at[layer, b], vbuf.at[b], v_sems.at[b])
-
-    def v_write(b):
-        return pltpu.make_async_copy(vbuf.at[b], v_out.at[layer, b], vo_sems.at[b])
+        return pltpu.make_async_copy(v_cache.at[layer, b], vbuf.at[b - held], v_sems.at[b])
 
     def k_write(b):
-        return pltpu.make_async_copy(keys.at[b], k_out.at[layer, b], ko_sems.at[b])
-
-    def k_patch(b):
-        return pltpu.make_async_copy(patch.at[b], k_out.at[layer, b, aligned(length(b)), :], p_sems.at[b])
-
-    def each(do):
+        return pltpu.make_async_copy(keys.at[b], k_out.at[layer, b], out_sems.at[0, b])
+
+    def v_write(b, held_group):
+        return pltpu.make_async_copy(value(b, held_group), v_out.at[layer, b], out_sems.at[1, b])
+
+    def put(i, b):
+        out = (k_out, v_out)[i]
+        return pltpu.make_async_copy(patch.at[i, b], out.at[layer, b, aligned(length(b)), :], patch_sems.at[i, b])
+
+    def each(do, first=0, last=MINE):
         def step(b, _):
             do(b)
             return 0
-        lax.fori_loop(0, MINE, step, 0)
-
-    each(lambda b: v_read(b).start())
+        lax.fori_loop(first, last, step, 0)
+
+    each(lambda b: v_read(b).start(), held, held + GRP)
     each(lambda b: k_write(b).start())
+    if held:
+        each(lambda b: v_write(b, True).start(), 0, held)
+    each(lambda b: v_read(b).start(), held + GRP, MINE)
     for i, r in enumerate((r0, r1, r2, r3)):
         qbuf[:, i * LH:(i + 1) * LH, :] = r[...].reshape(MINE, LH, HD)
     for b in range(MINE):
         new_kv[0, b] = k_new[b:b + 1, :].astype(F32)
         new_kv[1, b] = v_new[b:b + 1, :].astype(F32)
 
-    def context(seqs, size):
-        scores = []
+    def context(seqs, size, held_group):
+        scores, news = [], []
         for b in seqs:
             s = lax.dot_general(qbuf[b], keys[b, 0:size, :], (((1,), (1,)), ((), ())), preferred_element_type=F32)
-            s_new = jnp.sum(qbuf[b].astype(F32) * new_kv[0, b], axis=1, keepdims=True)
             pos = lax.broadcasted_iota(jnp.int32, (n_heads, size), 1)
-            s = jnp.where(pos == length(b), s_new, s)
-            scores.append(jnp.where(pos <= length(b), s * scale, -jnp.inf))
-        expos = [jnp.exp(s - jnp.max(s, axis=1, keepdims=True)) for s in scores]
-        probs = [(e * (1.0 / jnp.sum(e, axis=1, keepdims=True))).astype(BF16) for e in expos]
-        for b, p in zip(seqs, probs):
-            cbuf[b] = jnp.dot(p, vbuf[b, 0:size, :], preferred_element_type=F32).astype(BF16)
-
-    def long_one(b, _):
-        for n, size in enumerate(TIERS):
-            @pl.when(tier_of(b, n))
-            def _(size=size):
-                context((b,), size)
-        return 0
-
-    def group(g, _):
+            scores.append(jnp.where(pos < length(b), s * scale, -jnp.inf))
+            news.append(jnp.sum(qbuf[b].astype(F32) * new_kv[0, b], axis=1, keepdims=True) * scale)
+        tops = [jnp.maximum(jnp.max(s, axis=1, keepdims=True), n) for s, n in zip(scores, news)]
+        expos = [jnp.exp(s - t) for s, t in zip(scores, tops)]
+        news = [jnp.exp(n - t) for n, t in zip(news, tops)]
+        invs = [1.0 / (jnp.sum(e, axis=1, keepdims=True) + n) for e, n in zip(expos, news)]
+        probs = [(e * i).astype(BF16) for e, i in zip(expos, invs)]
+        news = [(n * i).astype(BF16).astype(F32) for n, i in zip(news, invs)]
+        for b, p, n in zip(seqs, probs, news):
+            old = jnp.dot(p, value(b, held_group)[0:size, :], preferred_element_type=F32)
+            cbuf[b] = (old + n * new_kv[1, b]).astype(BF16)
+
+    def settle_keys(b):
+        k_write(b).wait()
+        put(0, b).start()
+
+    def settle_values(b):
+        v_write(b, True).wait()
+        put(1, b).start()
+
+    def group(g, held_group):
         seqs = [g * GRP + i for i in range(GRP)]
         for b in seqs:
             rows = aligned(length(b))
-            patch[b] = with_row(keys[b, rows, :], length(b), new_kv[0, b].astype(BF16))
-            v_read(b).wait()
-            vbuf[b, rows, :] = with_row(vbuf[b, rows, :], length(b), new_kv[1, b].astype(BF16))
-        context(seqs, BLK)
-        for b in seqs:
-            v_write(b).start()
-            k_write(b).wait()
-            k_patch(b).start()
+            patch[0, b] = with_row(keys[b, rows, :], length(b), new_kv[0, b].astype(BF16))
+            if held_group:
+                patch[1, b] = with_row(value(b, True)[rows, :], length(b), new_kv[1, b].astype(BF16))
+            else:
+                v_read(b).wait()
+                value(b, False)[rows, :] = with_row(value(b, False)[rows, :], length(b), new_kv[1, b].astype(BF16))
+        if not held_group:
+            for b in seqs:
+                v_write(b, False).start()
+        context(seqs, BLK, held_group)
+        if g == MINE // GRP - 1:
+            each(settle_keys)
+            if held:
+                each(settle_values, 0, held)
+
+        def long_one(b, _):
+            for n, size in enumerate(TIERS):
+                @pl.when(tier_of(b, n))
+                def _(size=size):
+                    context((b,), size, held_group)
+            return 0
+
         lax.fori_loop(g * GRP, (g + 1) * GRP, long_one, 0)
-        return 0
-
-    lax.fori_loop(0, MINE // GRP, group, 0)
+
+    for g in range(MINE // GRP):
+        group(g, g < held // GRP)
     for i, c in enumerate((c0, c1, c2, c3)):
         c[...] = cbuf[:, i * LH:(i + 1) * LH, :].reshape(MINE, QW)
-    each(lambda b: v_write(b).wait())
-    each(lambda b: k_patch(b).wait())
-
-
-def attend(layer, lens, rs, k_new, v_new, keys, v_cache, priors):
-    args = [lens, *rs, k_new, v_new, keys, v_cache, *priors]
+    each(lambda b: v_write(b, False).wait(), held, MINE)
+    each(lambda b: put(0, b).wait())
+    if held:
+        each(lambda b: put(1, b).wait(), 0, held)
+
+
+def attend(layer, lens, rs, k_new, v_new, held, rest):
+    args = [lens, *rs, k_new, v_new, held, *rest]
     return pl.pallas_call(
         functools.partial(attend_kernel, layer, len(args)),
-        out_shape=[sds((MINE, QW))] * 4 + [sds(v_cache.shape)] * 2,
-        in_specs=[SSPEC] + [VSPEC] * 7 + [ASPEC] * (len(args) - 8),
+        out_shape=[sds((MINE, QW))] * 4 + [sds((2, MINE, SEQ, HD))] * 2,
+        in_specs=[SSPEC] + [VSPEC] * 7 + [ASPEC] * len(rest),
         out_specs=[VSPEC] * 4 + [ASPEC] * 2,
-        input_output_aliases={9: 4, 10: 5} if priors else {},
+        input_output_aliases={9: 4, 10: 5} if layer else {},
         scratch_shapes=[
-            VM((MINE, SEQ, HD), BF16),
             VM((MINE, GROUPS * LH, HD), BF16),
             VM((MINE, GROUPS * LH, HD), BF16),
             VM((2, MINE, 1, HD), F32),
-            VM((MINE, 16, HD), BF16),
-            pltpu.SemaphoreType.DMA((MINE,)),
-            pltpu.SemaphoreType.DMA((MINE,)),
-            pltpu.SemaphoreType.DMA((MINE,)),
+            VM((2, MINE, 16, HD), BF16),
+            pltpu.SemaphoreType.DMA((2, MINE)),
+            pltpu.SemaphoreType.DMA((2, MINE)),
+            VM((MINE - V_HELD[layer], SEQ, HD), BF16),
             pltpu.SemaphoreType.DMA((MINE,)),
         ],
-        compiler_params=pltpu.CompilerParams(vmem_limit_bytes=BIG),
+        compiler_params=pltpu.CompilerParams(vmem_limit_bytes=36 * MIB if layer else BIG),
         cost_estimate=pl.CostEstimate(flops=5_000_000_000, bytes_accessed=24 * MIB, transcendentals=0),
         name=f"attend_{layer}",
     )(*args)
@@ -305,9 +357,9 @@
 def out_kernel(layer, fuse, *refs):
     c_refs, (res, wo), refs = refs[:4], refs[4:6], refs[6:]
     if fuse:
-        (wq, wk, wv, k_cache), outs, refs = refs[:4], refs[4:12], refs[12:]
-        r_outs, (k_new, v_new, res_out, keys) = outs[:4], outs[4:]
-        hid, qbuf, acc, q_all, rbuf, q_sems, k_sems = refs[:7]
+        (wq, wk, wv, k_cache, v_cache), outs, refs = refs[:5], refs[5:13], refs[13:]
+        r_outs, (k_new, v_new, res_out, held) = outs[:4], outs[4:]
+        hid, qbuf, acc, q_all, rbuf, q_sems, kv_sems = refs[:7]
         refs = refs[7:]
     else:
         hid, refs = refs[0], refs[1:]
@@ -369,6 +421,10 @@
     def hidden(kind, j, owner, dev):
         part = hid.at[:, cols(owner * NJ + j)]
         return send(kind, j, part, part, dev)
+
+    def last_half(kind, p, owner, dev):
+        part = hid.at[:, pl.ds(pl.multiple_of(owner * QW + QW - CH + p * (CH // 2), CH // 2), CH // 2)]
+        return send(kind, NJ - 1 + p, part, part, dev)
 
     def start_wo(step, _):
         wo_copy(step).start()
@@ -487,7 +543,15 @@
         hid[:, cols(me * NJ + j)] = part
         if fuse:
             res_out[:, cols(j)] = part
-        hidden(4, j, me, cross).start()
+        @pl.when(j < NJ - 1)
+        def _():
+            hidden(4, j, me, cross).start()
+
+        @pl.when(j == NJ - 1)
+        def _():
+            last_half(4, 0, me, cross).start()
+            last_half(4, 1, me, cross).start()
+            last_half(5, 1, me, diag).start()
         hidden(3, j, me, partner).start()
         next_q(me, j, 2 * j)
 
@@ -499,13 +563,33 @@
     lax.fori_loop(0, NJ, phase_c, 0)
     from_partner(NJ - 1)
 
-    def forwarded(j):
-        hidden(5, j, diag, partner).wait_recv()
+    def forwarded(j, last=False):
+        if last:
+            last_half(5, 0, diag, partner).wait_recv()
+            last_half(5, 1, diag, diag).wait_recv()
+        else:
+            hidden(5, j, diag, partner).wait_recv()
         next_q(diag, j, 2 * NJ + 2 * j + 1)
 
+    def next_caches(act):
+        read_cache(MINE, k_cache.at[layer + 1], held, kv_sems.at[0], act)
+        read_cache(V_HELD[layer + 1], v_cache.at[layer + 1], held.at[pl.ds(MINE, V_HELD[layer + 1])], kv_sems.at[1], act)
+
     def phase_d(j, _):
-        hidden(4, j, cross, cross).wait_recv()
-        hidden(5, j, cross, partner).start()
+        if fuse:
+            @pl.when(j == CACHES_AT)
+            def _():
+                next_caches(lambda cp: cp.start())
+        @pl.when(j < NJ - 1)
+        def _():
+            hidden(4, j, cross, cross).wait_recv()
+            hidden(5, j, cross, partner).start()
+
+        @pl.when(j == NJ - 1)
+        def _():
+            last_half(4, 0, cross, cross).wait_recv()
+            last_half(5, 0, cross, partner).start()
+            last_half(4, 1, cross, cross).wait_recv()
         next_q(cross, j, 2 * NJ + 2 * j)
 
         @pl.when(j > 0)
@@ -514,9 +598,7 @@
         return 0
 
     lax.fori_loop(0, NJ, phase_d, 0)
-    if fuse:
-        read_keys(layer + 1, k_cache, keys, k_sems, lambda cp: cp.start())
-    forwarded(NJ - 1)
+    forwarded(NJ - 1, last=True)
 
     if fuse:
         def query(i):
@@ -534,7 +616,7 @@
         for i in (1, 2, 3):
             query(i).wait_recv()
             r_outs[i][...] = rbuf[i - 1]
-        read_keys(layer + 1, k_cache, keys, k_sems, lambda cp: cp.wait())
+        next_caches(lambda cp: cp.wait())
         for i in (1, 2, 3):
             query(i).wait_send()
     for i in (1, 2, 3):
@@ -546,11 +628,18 @@
             across(t).wait_send()
         pair_b(j).wait_send()
         hidden(3, j, me, partner).wait_send()
-        hidden(4, j, me, cross).wait_send()
-        hidden(5, j, cross, partner).wait_send()
+
+        @pl.when(j < NJ - 1)
+        def _():
+            hidden(4, j, me, cross).wait_send()
+            hidden(5, j, cross, partner).wait_send()
         return 0
 
     lax.fori_loop(0, NJ, drain, 0)
+    last_half(4, 0, me, cross).wait_send()
+    last_half(4, 1, me, cross).wait_send()
+    last_half(5, 0, cross, partner).wait_send()
+    last_half(5, 1, me, diag).wait_send()
 
 
 def out_product(layer, fuse, cs, res, w_out, qkv_weights):
@@ -567,7 +656,7 @@
     ]
     flops = 2 * ROWS * QW * D
     if fuse:
-        out_shape = [sds((MINE, QW))] * 4 + [sds((MINE, HD))] * 2 + [sds((ROWS, QW)), VM((MINE, SEQ, HD), BF16)]
+        out_shape = [sds((MINE, QW))] * 4 + [sds((MINE, HD))] * 2 + [sds((ROWS, QW)), VM((MINE + V_HELD[1], SEQ, HD), BF16)]
         out_specs = [VSPEC] * 8
         extra = [
             VM((ROWS, D), BF16),
@@ -576,7 +665,7 @@
             VM((ROWS, QW), BF16),
             VM((GROUPS - 1, MINE, QW), BF16),
             pltpu.SemaphoreType.DMA((3, Q_SLOTS)),
-            pltpu.SemaphoreType.DMA((MINE,)),
+            pltpu.SemaphoreType.DMA((2, MINE)),
         ]
         args = (*cs, res, w_out, *qkv_weights)
         flops += 2 * ROWS * D * QKV
@@ -592,7 +681,7 @@
         out_specs=out_specs,
         scratch_shapes=extra + shared,
         compiler_params=pltpu.CompilerParams(
-            vmem_limit_bytes=44 * MIB, collective_id=layer, has_side_effects=True),
+            vmem_limit_bytes=(39 if fuse else 44) * MIB, collective_id=layer, has_side_effects=True),
         cost_estimate=pl.CostEstimate(flops=flops, bytes_accessed=flops // ROWS, transcendentals=0),
         name=f"out_product_{layer}",
     )(*args)
@@ -602,11 +691,11 @@
     cache_spec = P(None, ("replica", "model"), None, None)
 
     def device_step(x, cache_len, w_query, w_key, w_value, w_out, k_cache, v_cache):
-        x = pltpu.with_memory_space_constraint(x, pltpu.HBM)
-        *rs, k_new, v_new, keys = first_qkv(x, w_query, w_key, w_value, k_cache)
-        *cs, k_out, v_out = attend(0, cache_len, rs, k_new, v_new, keys, v_cache, ())
-        *rs, k_new, v_new, res, keys = out_product(0, True, cs, x, w_out, (w_query, w_key, w_value, k_cache))
-        *cs, k_out, v_out = attend(1, cache_len, rs, k_new, v_new, keys, v_cache, (k_out, v_out))
+        x, w_key, w_value = (pltpu.with_memory_space_constraint(a, pltpu.HBM) for a in (x, w_key, w_value))
+        *rs, k_new, v_new, held = first_qkv(x, w_query, w_key, w_value, k_cache)
+        *cs, k_out, v_out = attend(0, cache_len, rs, k_new, v_new, held, (v_cache,))
+        *rs, k_new, v_new, res, held = out_product(0, True, cs, x, w_out, (w_query, w_key, w_value, k_cache, v_cache))
+        *cs, k_out, v_out = attend(1, cache_len, rs, k_new, v_new, held, (v_cache, k_out, v_out))
         out = out_product(1, False, cs, res, w_out, ())
         return out, k_out, v_out
 

time: 97.8 us -> 95.4 us (0.975); the launches traced: 98.1 us -> 94.2 us
  Pallas kernels: 96.5 us -> 92.6 us
    pallas_call x2, Pallas kernels: 58.1 us -> 56 us  [out_product(): pl.pallas_call(functools.partial(out_kernel, layer, fuse), out_shape=out_...]
    pallas_call x2, Pallas kernels: 20.6 us -> 18.8 us  [attend(): pl.pallas_call(functools.partial(attend_kernel, layer, len(args)), out_sh...]
where the time goes in v4:
time: 95.4 us; the launch traced here: 94.2 us
  Pallas kernels  92.6 us (97%)
  local copies, waits for them, and re-layouts  0.98 us (1%)
    pallas_call x2, Pallas kernels, out_product(): pl.pallas_call(functools.partial(out_kernel, layer, fuse), out_shape=out_...  56 us
    pallas_call x2, Pallas kernels, attend(): pl.pallas_call(functools.partial(attend_kernel, layer, len(args)), out_sh...  18.8 us
    pallas_call x1, Pallas kernels, first_qkv(): pl.pallas_call(first_qkv_kernel, out_shape=[sds((MINE, QW))] * 4 + [sds((...  17.7 us

profile of v4, /device:TPU:0, one launch (start us, length us, event | category | flops | bytes accessed | tf_op | source)
XLA Modules:
  0.0 94.2 jit_solution(12866899989706662404)
XLA Ops:
  0.6 0.0 copy-start
  0.6 17.7 %first_qkv.1 = (bf16[16,2048]{1,0:T(8,128)(2,1)S(1)}, bf16[16,2048]{1,0:T(8,128)(2,1)S(1)}, bf16[16,2048]{1,0:T(8,128)(2,1)S(1)}, bf16[16,2048]{1,0:T(8,128)(2,1...) custom-call(bf16[64,8192]{1,0:T(8,128)(2,1)} %refs_4_.1, ...), custom_call_target="tpu_custom_call" | custom-call | flops 2415919104 | bytes 37748736 | tf_op jit(solution)/shard_map/first_qkv/pallas_call | solution.py:181
  18.4 0.0 copy-done
  18.4 10.0 %attend_0.1 = (bf16[16,2048]{1,0:T(8,128)(2,1)S(1)}, bf16[16,2048]{1,0:T(8,128)(2,1)S(1)}, bf16[16,2048]{1,0:T(8,128)(2,1)S(1)}, bf16[16,2048]{1,0:T(8,128)(2,1)...) custom-call(s32[64]{0:T(128)S(1)} %copy-done, ...), custom_call_target="tpu_custom_call" | custom-call | flops 5000000000 | bytes 25165824 | tf_op jit(solution)/shard_map/attend_0/pallas_call | solution.py:335
  28.4 31.2 %out_product_0.1 = (bf16[16,2048]{1,0:T(8,128)(2,1)S(1)}, bf16[16,2048]{1,0:T(8,128)(2,1)S(1)}, bf16[16,2048]{1,0:T(8,128)(2,1)S(1)}, bf16[16,2048]{1,0:T(8,128)...) custom-call(bf16[16,2048]{1,0:T(8,128)(2,1)S(1)} %get-tuple-element., ...), custom_call_target="tpu_custom_call" | custom-call | flops 4563402752 | bytes 71303168 | tf_op jit(solution)/shard_map/out_product_0/pallas_call | solution.py:677
  59.6 8.8 %attend_1.1 = (bf16[16,2048]{1,0:T(8,128)(2,1)S(1)}, bf16[16,2048]{1,0:T(8,128)(2,1)S(1)}, bf16[16,2048]{1,0:T(8,128)(2,1)S(1)}, bf16[16,2048]{1,0:T(8,128)(2,1)...) custom-call(s32[64]{0:T(128)S(1)} %copy-done, ...), custom_call_target="tpu_custom_call", output_to_operand_aliasing={{4}: (9, {}), {5}: (10, {})} | custom-call | flops 5000000000 | bytes 25165824 | tf_op jit(solution)/shard_map/attend_1/pallas_call | solution.py:335
  68.5 24.8 %out_product_1.1 = bf16[64,8192]{1,0:T(8,128)(2,1)S(1)} custom-call(bf16[16,2048]{1,0:T(8,128)(2,1)S(1)} %get-tuple-element.50.refs_0_, bf16[16,2048]{1,0:T(8,128)(2,1)S(1)} %get-tuple-element.51.refs_1_, bf16[16,2048]{1,0:T(8,128)(2,1)S(1)} %get-tuple-element.52.refs_2_, bf16[16,2048]{1,0:T(8,128)(2,1)S(1)} %get-tuple-element.53.refs_3_, ...), custom_call_target="tpu_custom_call" | custom-call | flops 2147483648 | bytes 33554432 | tf_op jit(solution)/shard_map/out_product_1/pallas_call | solution.py:677
  93.2 1.0 %copy.16 = bf16[64,8192]{1,0:T(8,128)(2,1)} copy(bf16[64,8192]{1,0:T(8,128)(2,1)S(1)} %out_product_1.1) | data formatting | bytes 2097152
Async XLA Ops:
  0.6 17.8 %copy-start = (s32[64]{0:T(128)S(1)}, s32[64]{0:T(128)}, u32[]{:S(2)}) copy-start(s32[64]{0:T(128)} %refs_0_.3) | copy-start | bytes 772

commit v5 on v4

--- a/solution.py
+++ b/solution.py
@@ -256,11 +256,10 @@
             return 0
         lax.fori_loop(first, last, step, 0)
 
-    each(lambda b: v_read(b).start(), held, held + GRP)
-    each(lambda b: k_write(b).start())
+    each(lambda b: v_read(b).start(), held, MINE)
     if held:
+        each(lambda b: k_write(b).start())
         each(lambda b: v_write(b, True).start(), 0, held)
-    each(lambda b: v_read(b).start(), held + GRP, MINE)
     for i, r in enumerate((r0, r1, r2, r3)):
         qbuf[:, i * LH:(i + 1) * LH, :] = r[...].reshape(MINE, LH, HD)
     for b in range(MINE):
@@ -305,11 +304,13 @@
         if not held_group:
             for b in seqs:
                 v_write(b, False).start()
+        if not held:
+            for b in seqs:
+                k_write(b).start()
         context(seqs, BLK, held_group)
-        if g == MINE // GRP - 1:
+        if g == MINE // GRP - 1 and held:
             each(settle_keys)
-            if held:
-                each(settle_values, 0, held)
+            each(settle_values, 0, held)
 
         def long_one(b, _):
             for n, size in enumerate(TIERS):
@@ -322,6 +323,8 @@
 
     for g in range(MINE // GRP):
         group(g, g < held // GRP)
+    if not held:
+        each(settle_keys)
     for i, c in enumerate((c0, c1, c2, c3)):
         c[...] = cbuf[:, i * LH:(i + 1) * LH, :].reshape(MINE, QW)
     each(lambda b: v_write(b, False).wait(), held, MINE)

time: 95.4 us -> 94 us (0.985); the launches traced: 94.2 us -> 94 us
  no operation moved by 1% of the time
where the time goes in v5:
time: 94 us
  Pallas kernels  92.4 us (98%)
  local copies, waits for them, and re-layouts  0.98 us (1%)
    pallas_call x2, Pallas kernels, out_product(): pl.pallas_call(functools.partial(out_kernel, layer, fuse), out_shape=out_...  55.5 us
    pallas_call x2, Pallas kernels, attend(): pl.pallas_call(functools.partial(attend_kernel, layer, len(args)), out_sh...  19.1 us
    pallas_call x1, Pallas kernels, first_qkv(): pl.pallas_call(first_qkv_kernel, out_shape=[sds((MINE, QW))] * 4 + [sds((...  17.7 us

profile of v5, /device:TPU:0, one launch (start us, length us, event | category | flops | bytes accessed | tf_op | source)
XLA Modules:
  0.0 94.0 jit_solution(11937369483620220015)
XLA Ops:
  0.6 0.0 copy-start
  0.6 17.7 %first_qkv.1 = (bf16[16,2048]{1,0:T(8,128)(2,1)S(1)}, bf16[16,2048]{1,0:T(8,128)(2,1)S(1)}, bf16[16,2048]{1,0:T(8,128)(2,1)S(1)}, bf16[16,2048]{1,0:T(8,128)(2,1...) custom-call(bf16[64,8192]{1,0:T(8,128)(2,1)} %refs_4_.1, ...), custom_call_target="tpu_custom_call" | custom-call | flops 2415919104 | bytes 37748736 | tf_op jit(solution)/shard_map/first_qkv/pallas_call | solution.py:181
  18.4 0.0 copy-done
  18.4 10.2 %attend_0.1 = (bf16[16,2048]{1,0:T(8,128)(2,1)S(1)}, bf16[16,2048]{1,0:T(8,128)(2,1)S(1)}, bf16[16,2048]{1,0:T(8,128)(2,1)S(1)}, bf16[16,2048]{1,0:T(8,128)(2,1)...) custom-call(s32[64]{0:T(128)S(1)} %copy-done, ...), custom_call_target="tpu_custom_call" | custom-call | flops 5000000000 | bytes 25165824 | tf_op jit(solution)/shard_map/attend_0/pallas_call | solution.py:338
  28.6 30.7 %out_product_0.1 = (bf16[16,2048]{1,0:T(8,128)(2,1)S(1)}, bf16[16,2048]{1,0:T(8,128)(2,1)S(1)}, bf16[16,2048]{1,0:T(8,128)(2,1)S(1)}, bf16[16,2048]{1,0:T(8,128)...) custom-call(bf16[16,2048]{1,0:T(8,128)(2,1)S(1)} %get-tuple-element., ...), custom_call_target="tpu_custom_call" | custom-call | flops 4563402752 | bytes 71303168 | tf_op jit(solution)/shard_map/out_product_0/pallas_call | solution.py:680
  59.2 9.0 %attend_1.1 = (bf16[16,2048]{1,0:T(8,128)(2,1)S(1)}, bf16[16,2048]{1,0:T(8,128)(2,1)S(1)}, bf16[16,2048]{1,0:T(8,128)(2,1)S(1)}, bf16[16,2048]{1,0:T(8,128)(2,1)...) custom-call(s32[64]{0:T(128)S(1)} %copy-done, ...), custom_call_target="tpu_custom_call", output_to_operand_aliasing={{4}: (9, {}), {5}: (10, {})} | custom-call | flops 5000000000 | bytes 25165824 | tf_op jit(solution)/shard_map/attend_1/pallas_call | solution.py:338
  68.3 24.8 %out_product_1.1 = bf16[64,8192]{1,0:T(8,128)(2,1)S(1)} custom-call(bf16[16,2048]{1,0:T(8,128)(2,1)S(1)} %get-tuple-element.50.refs_0_, bf16[16,2048]{1,0:T(8,128)(2,1)S(1)} %get-tuple-element.51.refs_1_, bf16[16,2048]{1,0:T(8,128)(2,1)S(1)} %get-tuple-element.52.refs_2_, bf16[16,2048]{1,0:T(8,128)(2,1)S(1)} %get-tuple-element.53.refs_3_, ...), custom_call_target="tpu_custom_call" | custom-call | flops 2147483648 | bytes 33554432 | tf_op jit(solution)/shard_map/out_product_1/pallas_call | solution.py:680
  93.0 1.0 %copy.16 = bf16[64,8192]{1,0:T(8,128)(2,1)} copy(bf16[64,8192]{1,0:T(8,128)(2,1)S(1)} %out_product_1.1) | data formatting | bytes 2097152
Async XLA Ops:
  0.6 17.8 %copy-start = (s32[64]{0:T(128)S(1)}, s32[64]{0:T(128)}, u32[]{:S(2)}) copy-start(s32[64]{0:T(128)} %refs_0_.3) | copy-start | bytes 772

commit v6 on v5

--- a/solution.py
+++ b/solution.py
@@ -134,7 +134,7 @@
         qbuf[:, cols(n)] = acc[...].astype(BF16)
 
     def leave(n):
-        for i in (3, 2, 1):
+        for i in (2, 3, 1):
             send(i, n).start()
 
     group(0)
@@ -451,7 +451,7 @@
     for i in range(1, GROUPS):
         pl.semaphore_signal(barrier, inc=1, device_id={"model": xor_id(me, i)}, device_id_type=pl.DeviceIdType.MESH)
     pl.semaphore_wait(barrier, GROUPS - 1)
-    for i in (1, 2, 3):
+    for i in (2, 3, 1):
         context(i).start()
 
     def part_sum(step):
@@ -610,7 +610,7 @@
             return send(6, GROUPS + i, q_all.at[rows, :], rbuf.at[i - 1], dev)
 
         q_all[...] = acc[:, 0:QW].astype(BF16)
-        for i in (3, 2, 1):
+        for i in (2, 3, 1):
             query(i).start()
         mine = pl.ds(pl.multiple_of(me * MINE, MINE), MINE)
         k_new[...] = acc[mine, QW:QW + HD].astype(BF16)

time: 94 us -> 93.5 us (level)
  no operation moved by 1% of the time
where the time goes in v6:
time: 93.5 us; the launch traced here: 93.7 us
  Pallas kernels  92 us (98%)
  local copies, waits for them, and re-layouts  0.98 us (1%)
    pallas_call x2, Pallas kernels, out_product(): pl.pallas_call(functools.partial(out_kernel, layer, fuse), out_shape=out_...  54.8 us
    pallas_call x2, Pallas kernels, attend(): pl.pallas_call(functools.partial(attend_kernel, layer, len(args)), out_sh...  19.7 us
    pallas_call x1, Pallas kernels, first_qkv(): pl.pallas_call(first_qkv_kernel, out_shape=[sds((MINE, QW))] * 4 + [sds((...  17.6 us

profile of v6, /device:TPU:0, one launch (start us, length us, event | category | flops | bytes accessed | tf_op | source)
XLA Modules:
  0.0 93.7 jit_solution(16432638222483387397)
XLA Ops:
  0.6 0.0 copy-start
  0.6 17.6 %first_qkv.1 = (bf16[16,2048]{1,0:T(8,128)(2,1)S(1)}, bf16[16,2048]{1,0:T(8,128)(2,1)S(1)}, bf16[16,2048]{1,0:T(8,128)(2,1)S(1)}, bf16[16,2048]{1,0:T(8,128)(2,1...) custom-call(bf16[64,8192]{1,0:T(8,128)(2,1)} %refs_4_.1, ...), custom_call_target="tpu_custom_call" | custom-call | flops 2415919104 | bytes 37748736 | tf_op jit(solution)/shard_map/first_qkv/pallas_call | solution.py:181
  18.2 0.0 copy-done
  18.2 10.2 %attend_0.1 = (bf16[16,2048]{1,0:T(8,128)(2,1)S(1)}, bf16[16,2048]{1,0:T(8,128)(2,1)S(1)}, bf16[16,2048]{1,0:T(8,128)(2,1)S(1)}, bf16[16,2048]{1,0:T(8,128)(2,1)...) custom-call(s32[64]{0:T(128)S(1)} %copy-done, ...), custom_call_target="tpu_custom_call" | custom-call | flops 5000000000 | bytes 25165824 | tf_op jit(solution)/shard_map/attend_0/pallas_call | solution.py:338
  28.4 30.0 %out_product_0.1 = (bf16[16,2048]{1,0:T(8,128)(2,1)S(1)}, bf16[16,2048]{1,0:T(8,128)(2,1)S(1)}, bf16[16,2048]{1,0:T(8,128)(2,1)S(1)}, bf16[16,2048]{1,0:T(8,128)...) custom-call(bf16[16,2048]{1,0:T(8,128)(2,1)S(1)} %get-tuple-element., ...), custom_call_target="tpu_custom_call" | custom-call | flops 4563402752 | bytes 71303168 | tf_op jit(solution)/shard_map/out_product_0/pallas_call | solution.py:680
  58.4 9.5 %attend_1.1 = (bf16[16,2048]{1,0:T(8,128)(2,1)S(1)}, bf16[16,2048]{1,0:T(8,128)(2,1)S(1)}, bf16[16,2048]{1,0:T(8,128)(2,1)S(1)}, bf16[16,2048]{1,0:T(8,128)(2,1)...) custom-call(s32[64]{0:T(128)S(1)} %copy-done, ...), custom_call_target="tpu_custom_call", output_to_operand_aliasing={{4}: (9, {}), {5}: (10, {})} | custom-call | flops 5000000000 | bytes 25165824 | tf_op jit(solution)/shard_map/attend_1/pallas_call | solution.py:338
  67.9 24.8 %out_product_1.1 = bf16[64,8192]{1,0:T(8,128)(2,1)S(1)} custom-call(bf16[16,2048]{1,0:T(8,128)(2,1)S(1)} %get-tuple-element.50.refs_0_, bf16[16,2048]{1,0:T(8,128)(2,1)S(1)} %get-tuple-element.51.refs_1_, bf16[16,2048]{1,0:T(8,128)(2,1)S(1)} %get-tuple-element.52.refs_2_, bf16[16,2048]{1,0:T(8,128)(2,1)S(1)} %get-tuple-element.53.refs_3_, ...), custom_call_target="tpu_custom_call" | custom-call | flops 2147483648 | bytes 33554432 | tf_op jit(solution)/shard_map/out_product_1/pallas_call | solution.py:680
  92.7 1.0 %copy.16 = bf16[64,8192]{1,0:T(8,128)(2,1)} copy(bf16[64,8192]{1,0:T(8,128)(2,1)S(1)} %out_product_1.1) | data formatting | bytes 2097152
Async XLA Ops:
  0.6 17.6 %copy-start = (s32[64]{0:T(128)S(1)}, s32[64]{0:T(128)}, u32[]{:S(2)}) copy-start(s32[64]{0:T(128)} %refs_0_.3) | copy-start | bytes 772

commit v7 on v6

--- a/solution.py
+++ b/solution.py
@@ -68,6 +68,9 @@
 def first_qkv_kernel(x, wq, wk, wv, k_cache, r0, r1, r2, r3, k_new, v_new, keys,
                      xbuf, wbuf, kvbuf, acc, qbuf, rbuf, kvrows, kvback, x_sem, w_sems, kv_sems, k_sems, ssems, rsems):
     me = lax.axis_index("model")
+    barrier = pltpu.get_barrier_semaphore()
+    for i in range(1, GROUPS):
+        pl.semaphore_signal(barrier, inc=1, device_id={"model": xor_id(me, i)}, device_id_type=pl.DeviceIdType.MESH)
     depth = D // NJ
 
     def cols(n):
@@ -108,9 +111,6 @@
 
     lax.fori_loop(0, AHEAD, start, 0)
 
-    barrier = pltpu.get_barrier_semaphore()
-    for i in range(1, GROUPS):
-        pl.semaphore_signal(barrier, inc=1, device_id={"model": xor_id(me, i)}, device_id_type=pl.DeviceIdType.MESH)
     x_copy.wait()
 
     def group(n):
@@ -369,6 +369,9 @@
     ctx, resv, wbuf, send_a, recv_a, send_c, recv_c, send_b, recv_b, own, w_sems, res_sem, ssems, rsems = refs
 
     me = lax.axis_index("model")
+    barrier = pltpu.get_barrier_semaphore()
+    for i in range(1, GROUPS):
+        pl.semaphore_signal(barrier, inc=1, device_id={"model": xor_id(me, i)}, device_id_type=pl.DeviceIdType.MESH)
     n_wo = WO_SLOTS[layer]
     partner, cross, diag = xor_id(me, 1), xor_id(me, 2), xor_id(me, 3)
 
@@ -443,16 +446,14 @@
 
     ctx[pl.ds(pl.multiple_of(me * MINE, MINE), MINE), :] = c_refs[0][...]
     if fuse:
-        acc[...] = jnp.zeros_like(acc)
         for slot in range(Q_FIRST):
             start_q(slot)
 
-    barrier = pltpu.get_barrier_semaphore()
-    for i in range(1, GROUPS):
-        pl.semaphore_signal(barrier, inc=1, device_id={"model": xor_id(me, i)}, device_id_type=pl.DeviceIdType.MESH)
     pl.semaphore_wait(barrier, GROUPS - 1)
     for i in (2, 3, 1):
         context(i).start()
+    if fuse:
+        acc[...] = jnp.zeros_like(acc)
 
     def part_sum(step):
         wo_copy(step).wait()

time: 93.5 us -> 93.3 us (level)
  Pallas kernels: 92 us -> 90.9 us
where the time goes in v7:
time: 93.3 us; the launch traced here: 92.6 us
  Pallas kernels  90.9 us (97%)
  local copies, waits for them, and re-layouts  0.98 us (1%)
    pallas_call x2, Pallas kernels, out_product(): pl.pallas_call(functools.partial(out_kernel, layer, fuse), out_shape=out_...  54.3 us
    pallas_call x2, Pallas kernels, attend(): pl.pallas_call(functools.partial(attend_kernel, layer, len(args)), out_sh...  19 us
    pallas_call x1, Pallas kernels, first_qkv(): pl.pallas_call(first_qkv_kernel, out_shape=[sds((MINE, QW))] * 4 + [sds((...  17.6 us

profile of v7, /device:TPU:0, one launch (start us, length us, event | category | flops | bytes accessed | tf_op | source)
XLA Modules:
  0.0 92.6 jit_solution(7347381378241410922)
XLA Ops:
  0.6 0.0 copy-start
  0.6 17.6 %first_qkv.1 = (bf16[16,2048]{1,0:T(8,128)(2,1)S(1)}, bf16[16,2048]{1,0:T(8,128)(2,1)S(1)}, bf16[16,2048]{1,0:T(8,128)(2,1)S(1)}, bf16[16,2048]{1,0:T(8,128)(2,1...) custom-call(bf16[64,8192]{1,0:T(8,128)(2,1)} %refs_4_.1, ...), custom_call_target="tpu_custom_call" | custom-call | flops 2415919104 | bytes 37748736 | tf_op jit(solution)/shard_map/first_qkv/pallas_call | solution.py:181
  18.2 0.0 copy-done
  18.2 10.2 %attend_0.1 = (bf16[16,2048]{1,0:T(8,128)(2,1)S(1)}, bf16[16,2048]{1,0:T(8,128)(2,1)S(1)}, bf16[16,2048]{1,0:T(8,128)(2,1)S(1)}, bf16[16,2048]{1,0:T(8,128)(2,1)...) custom-call(s32[64]{0:T(128)S(1)} %copy-done, ...), custom_call_target="tpu_custom_call" | custom-call | flops 5000000000 | bytes 25165824 | tf_op jit(solution)/shard_map/attend_0/pallas_call | solution.py:338
  28.4 30.0 %out_product_0.1 = (bf16[16,2048]{1,0:T(8,128)(2,1)S(1)}, bf16[16,2048]{1,0:T(8,128)(2,1)S(1)}, bf16[16,2048]{1,0:T(8,128)(2,1)S(1)}, bf16[16,2048]{1,0:T(8,128)...) custom-call(bf16[16,2048]{1,0:T(8,128)(2,1)S(1)} %get-tuple-element., ...), custom_call_target="tpu_custom_call" | custom-call | flops 4563402752 | bytes 71303168 | tf_op jit(solution)/shard_map/out_product_0/pallas_call | solution.py:681
  58.4 8.8 %attend_1.1 = (bf16[16,2048]{1,0:T(8,128)(2,1)S(1)}, bf16[16,2048]{1,0:T(8,128)(2,1)S(1)}, bf16[16,2048]{1,0:T(8,128)(2,1)S(1)}, bf16[16,2048]{1,0:T(8,128)(2,1)...) custom-call(s32[64]{0:T(128)S(1)} %copy-done, ...), custom_call_target="tpu_custom_call", output_to_operand_aliasing={{4}: (9, {}), {5}: (10, {})} | custom-call | flops 5000000000 | bytes 25165824 | tf_op jit(solution)/shard_map/attend_1/pallas_call | solution.py:338
  67.2 24.3 %out_product_1.1 = bf16[64,8192]{1,0:T(8,128)(2,1)S(1)} custom-call(bf16[16,2048]{1,0:T(8,128)(2,1)S(1)} %get-tuple-element.50.refs_0_, bf16[16,2048]{1,0:T(8,128)(2,1)S(1)} %get-tuple-element.51.refs_1_, bf16[16,2048]{1,0:T(8,128)(2,1)S(1)} %get-tuple-element.52.refs_2_, bf16[16,2048]{1,0:T(8,128)(2,1)S(1)} %get-tuple-element.53.refs_3_, ...), custom_call_target="tpu_custom_call" | custom-call | flops 2147483648 | bytes 33554432 | tf_op jit(solution)/shard_map/out_product_1/pallas_call | solution.py:681
  91.6 1.0 %copy.16 = bf16[64,8192]{1,0:T(8,128)(2,1)} copy(bf16[64,8192]{1,0:T(8,128)(2,1)S(1)} %out_product_1.1) | data formatting | bytes 2097152
Async XLA Ops:
  0.6 17.6 %copy-start = (s32[64]{0:T(128)S(1)}, s32[64]{0:T(128)}, u32[]{:S(2)}) copy-start(s32[64]{0:T(128)} %refs_0_.3) | copy-start | bytes 772
